TPU v7x, 32 devices: a 4x4x1 block of a 4x4x8 slice. The times are simulated.
32 devices in a mesh: batch: 1 (over z), col: 4 (over y), row: 8 (over x, core).
Axes of the slice: x: 4, y: 4, z: 1, core: 2. Of those that a mesh axis runs over, the one named last changes fastest.
The devices are a block of a 4x4x8 slice.
Arguments:
- pair_rep: bfloat16 [768, 768, 128], P(('batch', 'row'), 'col')
- pair_mask: int32 [768, 768], P(('batch', 'row'), 'col')
- ln_in_scale: bfloat16 [128], replicated
- w_left: bfloat16 [128, 128], replicated
- w_left_gate: bfloat16 [128, 128], replicated
- w_right: bfloat16 [128, 128], replicated
- w_right_gate: bfloat16 [128, 128], replicated
- w_out_gate: bfloat16 [128, 128], replicated
- ln_out_scale: bfloat16 [128], replicated
- w_out: bfloat16 [128, 128], replicated
Outputs:
- output: bfloat16 [768, 768, 128], P(('batch', 'row'), 'col')
All inputs are finite; a program needn't handle non-finite values.
Results may differ from a plain program's by a relative error of at most 0.00117811.
Values are sent between devices in bfloat16 or wider.
A program may use at most 768 MiB of HBM per device.

v0:
```python
import jax
import jax.numpy as jnp
from jax import lax
from jax.sharding import PartitionSpec as P

LN_EPS = 0.00001


def layer_norm(values, gain_vec):
    mean_val = jnp.mean(values, axis=-1, keepdims=True)
    centered = values - mean_val
    variance = jnp.mean(centered * centered, axis=-1, keepdims=True)
    return centered * lax.rsqrt(variance + LN_EPS) * gain_vec.astype(jnp.float32)


def project_tile(pair_tile, mask_tile, ln_in_scale, w_left, w_left_gate, w_right, w_right_gate, w_out_gate):
    tri_dim = w_left.shape[1]
    normed = layer_norm(pair_tile.astype(jnp.float32), ln_in_scale).astype(jnp.bfloat16)
    w_cat = jnp.concatenate([w_left, w_left_gate, w_right, w_right_gate, w_out_gate], axis=1)
    proj_all = jnp.einsum('ijz,zh->ijh', normed, w_cat, preferred_element_type=jnp.float32)
    keep_mask = mask_tile.astype(jnp.float32)[:, :, None]
    left_act = (keep_mask * jax.nn.sigmoid(proj_all[:, :, tri_dim:2 * tri_dim]) * proj_all[:, :, :tri_dim]).astype(jnp.bfloat16)
    right_act = (keep_mask * jax.nn.sigmoid(proj_all[:, :, 3 * tri_dim:4 * tri_dim]) * proj_all[:, :, 2 * tri_dim:3 * tri_dim]).astype(jnp.bfloat16)
    gate_act = jax.nn.sigmoid(proj_all[:, :, 4 * tri_dim:])
    return left_act, right_act, gate_act


def finish_tile(normed_out, pair_tile, gate_act, w_out):
    update = jnp.einsum('ijh,hz->ijz', normed_out, w_out, preferred_element_type=jnp.float32)
    return (pair_tile.astype(jnp.float32) + gate_act * update).astype(jnp.bfloat16)


def solution(mesh):
    row_count = mesh.shape['row']
    col_count = mesh.shape['col']
    tile_spec = P(('batch', 'row'), 'col', None)
    mask_spec = P(('batch', 'row'), 'col')
    replicated = P()

    def local_step(pair_tile, mask_tile, ln_in_scale, w_left, w_left_gate, w_right, w_right_gate, w_out_gate, ln_out_scale, w_out):
        left_act, right_act, gate_act = project_tile(pair_tile, mask_tile, ln_in_scale, w_left, w_left_gate, w_right, w_right_gate, w_out_gate)
        tile_rows, tile_cols, tri_dim = left_act.shape
        sub_len = tile_rows // col_count
        moved_a = lax.all_to_all(left_act, 'col', 0, 1, tiled=True)
        moved_a = lax.all_to_all(moved_a, 'row', 1, 0, tiled=True)
        left_panel = lax.all_gather(moved_a, 'col', axis=0, tiled=True).reshape(col_count, row_count, sub_len, tile_rows, tri_dim)
        right_panel = lax.all_gather(right_act, 'row', axis=0, tiled=True).reshape(row_count, col_count, sub_len, tile_cols, tri_dim)
        summed = jnp.einsum('ursih,rusjh->ijh', left_panel, right_panel, preferred_element_type=jnp.float32)
        normed_out = layer_norm(summed, ln_out_scale).astype(jnp.bfloat16)
        return finish_tile(normed_out, pair_tile, gate_act, w_out)

    return jax.shard_map(local_step, mesh=mesh, in_specs=(tile_spec, mask_spec) + (replicated,) * 8, out_specs=tile_spec, check_vma=False)
```

profile of v0, /device:TPU:101, one launch (start us, length us, event | category | flops | bytes accessed | tf_op | source)
XLA Modules:
  0.0 662.6 jit_solution(830771365693723229)
XLA Ops:
  6.5 0.0 copy-start
  6.6 0.0 copy-start.3
  6.6 0.0 copy-start.8
  6.6 0.0 copy-start.2
  6.6 0.0 copy-start.4
  6.6 0.0 copy-start.5
  6.6 0.0 copy-start.6
  6.6 0.0 copy-start.7
  6.6 0.1 all-gather.5.cloned.1.call-start
  6.7 0.0 copy-start.1
  6.7 4.3 convert_reduce_fusion
  11.0 7.7 %fusion.2 = f32[96,192]{1,0:T(8,128)S(1)} fusion(bf16[96,192,128]{2,1,0:T(8,128)(2,1)} %param.10, f32[96,192]{1,0:T(8,128)S(1)} %broadcast_multiply_fusion.1), kind=kLoop, calls=%fused_computation.9 | loop fusion | flops 9418752 | bytes 4866048 | tf_op jit(solution)/shard_map/reduce_sum | solution.py:12
  18.7 0.0 copy-done.3
  18.7 0.0 copy-done.8
  18.7 0.0 copy-done.2
  18.8 0.0 copy-done.4
  18.8 0.0 copy-done.5
  18.8 0.0 copy-done.6
  18.8 0.0 copy-done.7
  18.9 0.0 copy-done.1
  18.9 16.4 %fusion.20 = f32[96,192,640]{2,1,0:T(8,128)} fusion(bf16[96,192,128]{2,1,0:T(8,128)(2,1)S(1)} %copy-done.1, f32[128]{0:T(128)S(1)} %convert_element_type.29, f32[96,192]{1,0:T(8,128)S(1)} %add_rsqrt_fusion.1, f32[96,192]{1,0:T(8,128)S(1)} %broadcast_multiply_fusion.1, bf16[128,640]{1,0:T(8,128)(2,1)S(1)} %constant_dynamic-update-slice_fusion), kind=kOutput, calls=%fused_computation.32 | convolution fusion | flops 3031695360 | bytes 52216320 | tf_op jit(solution)/shard_map/ijz,zh->ijh/dot_general | solution.py:20
  35.3 15.9 %fusion.6 = (bf16[96,192,128]{2,1,0:T(8,128)(2,1)S(1)}, bf16[96,192,128]{2,1,0:T(8,128)(2,1)}) fusion(f32[96,192,640]{2,1,0:T(8,128)} %fusion.20, f32[96,192]{1,0:T(8,128)S(1)} %convert_element_type.31), kind=kLoop, calls=%fused_computation.14 | loop fusion | flops 28311552 | bytes 47259648 | tf_op jit(solution)/shard_map/convert_element_type | solution.py:22
  51.2 58.9 %all_to_all.36 = bf16[96,192,128]{2,1,0:T(8,128)(2,1)S(1)} all-to-all(bf16[96,192,128]{2,1,0:T(8,128)(2,1)S(1)} %get-tuple-element.5), channel_id=1, replica_groups=mesh['batch'=1,'col'=4,'row'=8] {'col'}, dimensions={0} | all-to-all | bytes 9437184 | tf_op jit(solution)/shard_map/all_to_all | solution.py:44
  110.1 0.4 copy.46
  110.6 3.0 copy.47
  113.6 58.1 %all_to_all.37 = bf16[24,768,128]{2,0,1:T(8,128)(2,1)S(1)} all-to-all(bf16[24,768,128]{2,0,1:T(8,128)(2,1)S(1)} %copy.47), channel_id=1, replica_groups=mesh['batch'=1,'col'=4,'row'=8] {'row'}, dimensions={1} | all-to-all | bytes 9437184 | tf_op jit(solution)/shard_map/all_to_all | solution.py:45
  171.8 0.0 copy-start.9
  171.8 3.1 copy.49
  174.9 0.1 all-gather.5.cloned.1.call-update
  174.9 0.2 all-gather.3.cloned.1.call-start
  175.2 0.6 all-gather.3.cloned.1.call-update
  175.7 0.0 copy-done.9
  175.7 170.0 %all-gather.5.cloned.1.call-done = bf16[768,96,128]{2,1,0:T(8,128)(2,1)} async-done(((bf16[192,96,128]{2,1,0:T(8,128)(2,1)}), bf16[768,96,128]{2,1,0:T(8,128)(2,1)}) %all-gather.5.cloned.1.call-update) | async-done | bytes 18874384 | tf_op jit(solution)/shard_map/all_gather | solution.py:46
  345.7 29.6 %copy.51 = bf16[4,8,24,96,128]{3,2,0,1,4:T(8,128)(2,1)} copy(bf16[4,8,24,96,128]{4,3,2,1,0:T(8,128)(2,1)} %bitcast.35) | data formatting | bytes 37748736 | tf_op jit(solution)/shard_map/reshape | solution.py:46
  375.3 144.1 %all-gather.3.cloned.1.call-done = bf16[768,192,128]{2,1,0:T(8,128)(2,1)} async-done(((bf16[96,192,128]{2,1,0:T(8,128)(2,1)}), bf16[768,192,128]{2,1,0:T(8,128)(2,1)}) %all-gather.3.cloned.1.call-update) | async-done | bytes 37748752 | tf_op jit(solution)/shard_map/all_gather | solution.py:47
  519.3 67.3 %copy.50 = bf16[8,4,24,192,128]{3,2,1,0,4:T(8,128)(2,1)} copy(bf16[8,4,24,192,128]{4,3,2,1,0:T(8,128)(2,1)} %bitcast.30) | data formatting | bytes 75497472 | tf_op jit(solution)/shard_map/reshape | solution.py:47
  586.7 31.9 %bitcast_reduce_fusion = (f32[96,192]{0,1:T(8,128)S(1)}, f32[128,192,96,1,1]{2,1,4,3,0:T(8,128)}) fusion(bf16[8,4,24,192,128]{3,2,1,0,4:T(8,128)(2,1)} %copy.50, bf16[4,8,24,96,128]{3,2,0,1,4:T(8,128)(2,1)} %copy.51), kind=kOutput, calls=%fused_computation.4 | convolution fusion | flops 3626219520 | bytes 66134016 | tf_op jit(solution)/shard_map/ursih,rusjh->ijh/dot_general | solution.py:48
  618.6 0.1 copy.52
  618.7 0.1 copy.53
  618.8 6.3 multiply_reduce_fusion
  625.1 0.1 copy.54
  625.2 0.1 copy.55
  625.3 9.5 %multiply_convert_fusion = bf16[96,192,128]{0,1,2:T(8,128)(2,1)} fusion(f32[128,192,96,1,1]{2,1,4,3,0:T(8,128)} %get-tuple-element.8, f32[128]{0:T(128)S(1)} %convert_element_type.34, f32[96,192]{0,1:T(8,128)S(1)} %copy.55, f32[96,192]{0,1:T(8,128)S(1)} %copy.53), kind=kLoop, calls=%fused_computation.5 | loop fusion | flops 9437184 | bytes 14303744 | tf_op jit(solution)/shard_map/convert_element_type | solution.py:49
  634.8 9.3 %copy.56 = bf16[96,192,128]{2,1,0:T(8,128)(2,1)} copy(bf16[96,192,128]{0,1,2:T(8,128)(2,1)} %multiply_convert_fusion) | data formatting | bytes 9437184 | tf_op jit(solution)/shard_map/convert_element_type | solution.py:49
  644.1 0.0 copy-done
  644.1 11.6 %fusion.5 = bf16[96,192,128]{2,1,0:T(8,128)(2,1)} fusion(bf16[96,192,128]{2,1,0:T(8,128)(2,1)} %param.10, f32[96,192,640]{2,1,0:T(8,128)} %fusion.20, bf16[96,192,128]{2,1,0:T(8,128)(2,1)} %copy.56, bf16[128,128]{1,0:T(8,128)(2,1)S(1)} %copy-done), kind=kOutput, calls=%fused_computation.12 | convolution fusion | flops 620494848 | bytes 23625728 | tf_op jit(solution)/shard_map/ijh,hz->ijz/dot_general | solution.py:29
  (12 shorter events, 0.1 us)
Async XLA Ops:
  6.5 637.5 %copy-start = (bf16[128,128]{1,0:T(8,128)(2,1)S(1)}, bf16[128,128]{1,0:T(8,128)(2,1)}, u32[]{:S(2)}) copy-start(bf16[128,128]{1,0:T(8,128)(2,1)} %param.19) | copy-start | bytes 98308
  6.6 12.1 %copy-start.3 = (bf16[128,128]{1,0:T(8,128)(2,1)S(1)}, bf16[128,128]{1,0:T(8,128)(2,1)}, u32[]{:S(2)}) copy-start(bf16[128,128]{1,0:T(8,128)(2,1)} %param.13) | copy-start | bytes 98308
  6.6 12.2 %copy-start.8 = (bf16[128]{0:T(256)(128)(2,1)S(1)}, bf16[128]{0:T(256)(128)(2,1)}, u32[]{:S(2)}) copy-start(bf16[128]{0:T(256)(128)(2,1)} %param.12) | copy-start | bytes 772
  6.6 12.2 %copy-start.2 = (s32[96,192]{1,0:T(8,128)S(1)}, s32[96,192]{1,0:T(8,128)}, u32[]{:S(2)}) copy-start(s32[96,192]{1,0:T(8,128)} %param.11) | copy-start | bytes 221188
  6.6 12.2 %copy-start.4 = (bf16[128,128]{1,0:T(8,128)(2,1)S(1)}, bf16[128,128]{1,0:T(8,128)(2,1)}, u32[]{:S(2)}) copy-start(bf16[128,128]{1,0:T(8,128)(2,1)} %param.14) | copy-start | bytes 98308
  6.6 12.2 %copy-start.5 = (bf16[128,128]{1,0:T(8,128)(2,1)S(1)}, bf16[128,128]{1,0:T(8,128)(2,1)}, u32[]{:S(2)}) copy-start(bf16[128,128]{1,0:T(8,128)(2,1)} %param.15) | copy-start | bytes 98308
  6.6 12.2 %copy-start.6 = (bf16[128,128]{1,0:T(8,128)(2,1)S(1)}, bf16[128,128]{1,0:T(8,128)(2,1)}, u32[]{:S(2)}) copy-start(bf16[128,128]{1,0:T(8,128)(2,1)} %param.16) | copy-start | bytes 98308
  6.6 12.3 %copy-start.7 = (bf16[128,128]{1,0:T(8,128)(2,1)S(1)}, bf16[128,128]{1,0:T(8,128)(2,1)}, u32[]{:S(2)}) copy-start(bf16[128,128]{1,0:T(8,128)(2,1)} %param.17) | copy-start | bytes 98308
  6.6 339.1 %all-gather.5.cloned.1.call-start = ((), (), s32[]{:S(2)}) async-start(), calls=%async_computation.3 | async-start | bytes 23592960 | tf_op jit(solution)/shard_map/all_gather | solution.py:46
  6.7 12.2 %copy-start.1 = (bf16[96,192,128]{2,1,0:T(8,128)(2,1)S(1)}, bf16[96,192,128]{2,1,0:T(8,128)(2,1)}, u32[]{:S(2)}) copy-start(bf16[96,192,128]{2,1,0:T(8,128)(2,1)} %param.10) | copy-start | bytes 14155780
  171.8 4.0 copy-start.9
  174.9 344.4 %all-gather.3.cloned.1.call-start = ((), (), s32[]{:S(2)}) async-start(), calls=%async_computation.2 | async-start | bytes 42467328 | tf_op jit(solution)/shard_map/all_gather | solution.py:47
Sparse Core Ops, SparseCore 0:
  175.0 170.6 all-gather.4
  347.3 171.9 all-gather.2
where the time goes:
time: 668 us; the launch traced here: 663 us
  waiting for transfers between devices  315 us (47%)
  blocking collectives  117 us (18%)
  local copies, waits for them, and re-layouts  113 us (17%)
  matrix products  60 us (9%)
  other arithmetic  43.7 us (7%)
  between operations  13.7 us (2%)
    all_gather x1, waiting for transfers between devices, local_step(): lax.all_gather(moved_a, 'col', axis=0, tiled=True)  170 us
    all_gather x1, waiting for transfers between devices, local_step(): lax.all_gather(right_act, 'row', axis=0, tiled=True)  144 us
    reshape x1, local copies, waits for them, and re-layouts, local_step(): lax.all_gather(right_act, 'row', axis=0, tiled=True)  67.3 us
    all_to_all x1, blocking collectives, local_step(): moved_a = lax.all_to_all(left_act, 'col', 0, 1, tiled=True)  58.9 us
    all_to_all x1, blocking collectives, local_step(): moved_a = lax.all_to_all(moved_a, 'row', 1, 0, tiled=True)  58.1 us
    dot_general x1, matrix products, local_step(): jnp.einsum('ursih,rusjh->ijh', left_panel, right_panel, preferred_element...  31.9 us
    reshape x1, local copies, waits for them, and re-layouts, local_step(): lax.all_gather(moved_a, 'col', axis=0, tiled=True)  29.6 us
    dot_general x1, matrix products, project_tile(): jnp.einsum('ijz,zh->ijh', normed, w_cat, preferred_element_type=jnp.float32)  16.4 us
  transfers between devices with their start and end apart: 2, of which 2 were waited for; matrix products, arithmetic and copies ran while one was open for 4% of the time, Pallas kernels for 0%

commit v1 on v0

v1 whole, which is shorter than its diff:
```python
import functools

import jax
import jax.numpy as jnp
from jax import lax
from jax.experimental import pallas as pl
from jax.experimental.pallas import tpu as pltpu
from jax.sharding import PartitionSpec as P

LN_EPS = 0.00001
LANES = 128
HALF = 64
GROUP = 16
PITCH = 24
F32 = jnp.float32
BF16 = jnp.bfloat16


def dot(lhs, rhs, dims):
    return lax.dot_general(lhs, rhs, (dims, ((), ())), preferred_element_type=F32)


def layer_norm(values, gain):
    mean = jnp.mean(values, axis=-1, keepdims=True)
    centered = values - mean
    variance = jnp.mean(centered * centered, axis=-1, keepdims=True)
    return centered * lax.rsqrt(variance + LN_EPS) * gain


def project_kernel(z_ref, m_ref, g_ref, w_ref, x_ref, a_ref, b_ref, scr):
    heads = a_ref.shape[0]
    gain = g_ref[...].astype(F32)
    flat = scr.reshape(6 * heads * PITCH, LANES)

    def row(t, carry):
        lo = layer_norm(z_ref[0, t].astype(F32), gain).astype(BF16)
        hi = layer_norm(z_ref[1, t].astype(F32), gain).astype(BF16)
        x_ref[0, t] = lo
        x_ref[1, t] = hi
        parts = (lo[:LANES], hi[:LANES], jnp.concatenate([lo[LANES:], hi[LANES:]], axis=0))
        mask = m_ref[0, t].astype(F32)
        for seg in range(3):
            keep = mask[seg:seg + 1]
            for side in range(2):
                both = dot(w_ref[2 * side * heads:2 * (side + 1) * heads], parts[seg], ((1,), (1,)))
                act = keep * jax.nn.sigmoid(both[heads:]) * both[:heads]
                flat[pl.ds((2 * seg + side) * heads * PITCH + t, heads, stride=PITCH), :] = act
        return carry

    lax.fori_loop(0, GROUP, row, 0)

    def pack(h, carry):
        for seg in range(3):
            a_ref[h, seg] = scr[2 * seg * heads + h, 0:GROUP].astype(BF16)
            b_ref[h, seg] = scr[(2 * seg + 1) * heads + h, 0:GROUP].astype(BF16)
        return carry

    lax.fori_loop(0, heads, pack, 0)


def project(pair, mask, gain, weights):
    rows, cols, chan = pair.shape
    half = rows // 2
    heads = weights.shape[0] // 4
    steps = half // GROUP
    m = mask.reshape(2, half, cols)
    tail = jnp.concatenate([m[0, :, LANES:], m[1, :, LANES:]], axis=-1)
    m = jnp.stack([m[0, :, :LANES], m[1, :, :LANES], tail], axis=1)
    m = jnp.pad(m, ((0, 0), (0, 5), (0, 0))).reshape(steps, GROUP, 8, LANES)
    wire = jax.ShapeDtypeStruct((heads, 3, half, LANES), BF16)
    wire_spec = pl.BlockSpec((heads, 3, GROUP, LANES), lambda t: (0, 0, t, 0))
    tile_spec = pl.BlockSpec((2, GROUP, cols, chan), lambda t: (0, t, 0, 0))
    return pl.pallas_call(
        project_kernel,
        grid=(steps,),
        in_specs=[
            tile_spec,
            pl.BlockSpec((1, GROUP, 8, LANES), lambda t: (t, 0, 0, 0)),
            pl.BlockSpec((1, chan), lambda t: (0, 0)),
            pl.BlockSpec(weights.shape, lambda t: (0, 0)),
        ],
        out_specs=[tile_spec, wire_spec, wire_spec],
        out_shape=[jax.ShapeDtypeStruct((2, half, cols, chan), BF16), wire, wire],
        scratch_shapes=[pltpu.VMEM((6 * heads, PITCH, LANES), F32)],
        compiler_params=pltpu.CompilerParams(vmem_limit_bytes=60 * 2**20),
        cost_estimate=pl.CostEstimate(flops=2 * rows * cols * chan * 4 * heads, bytes_accessed=rows * cols * chan * 8, transcendentals=0),
    )(pair.reshape(2, half, cols, chan), m, gain.reshape(1, chan), weights)


def finish_kernel(y_ref, x_ref, z_ref, wg_ref, wo_ref, out_ref):
    srcs, _, _, per, _ = y_ref.shape
    heads = srcs * per

    def update(pos):
        return dot(y_ref[:, 0, pos].reshape(heads, LANES), wo_ref[...], ((0,), (0,)))

    def gated(x, z, upd):
        gate = jax.nn.sigmoid(dot(x, wg_ref[...], ((1,), (0,))))
        return (z.astype(F32) + gate * upd).astype(BF16)

    def wide(t, carry):
        out_ref[t, :LANES] = gated(x_ref[t, :LANES], z_ref[t, :LANES], update(t))
        return carry

    def narrow(t, carry):
        x = jnp.concatenate([x_ref[t, LANES:], x_ref[t + 16, LANES:]], axis=0)
        z = jnp.concatenate([z_ref[t, LANES:], z_ref[t + 16, LANES:]], axis=0)
        res = gated(x, z, update(t + 32))
        out_ref[t, LANES:] = res[:HALF]
        out_ref[t + 16, LANES:] = res[HALF:]
        return carry

    lax.fori_loop(0, 32, wide, 0, unroll=2)
    lax.fori_loop(0, 16, narrow, 0, unroll=2)


def finish(y, x, z, w_gate, w_out):
    rows, cols, chan = z.shape
    srcs, groups, places, per, _ = y.shape
    tile_spec = pl.BlockSpec((32, cols, chan), lambda t: (t, 0, 0))
    return pl.pallas_call(
        finish_kernel,
        grid=(groups,),
        in_specs=[
            pl.BlockSpec((srcs, 1, places, per, LANES), lambda t: (0, t, 0, 0, 0)),
            tile_spec,
            tile_spec,
            pl.BlockSpec(w_gate.shape, lambda t: (0, 0)),
            pl.BlockSpec(w_out.shape, lambda t: (0, 0)),
        ],
        out_specs=tile_spec,
        out_shape=jax.ShapeDtypeStruct(z.shape, BF16),
        compiler_params=pltpu.CompilerParams(vmem_limit_bytes=60 * 2**20),
        cost_estimate=pl.CostEstimate(flops=4 * rows * cols * chan * chan, bytes_accessed=rows * cols * chan * 8, transcendentals=0),
    )(y, x.reshape(z.shape), z, w_gate, w_out)


def exchange(a, b, gain, row_count, col_count):
    heads, _, half, _ = a.shape
    per = heads // row_count
    wire = (row_count, per, 3, half, LANES)
    got_a = lax.all_to_all(a.reshape(wire), 'row', 0, 0, tiled=True)
    all_a = lax.all_gather(got_a, 'col', axis=0)
    got_b = lax.all_to_all(b.reshape(wire), 'row', 0, 0, tiled=True)

    def unpack(w):
        w = jnp.moveaxis(w, -3, 0)
        tail = jnp.stack([w[2, ..., :HALF], w[2, ..., HALF:]])
        return jnp.concatenate([w[:2], tail], axis=-1)

    left, right = unpack(all_a), unpack(got_b)
    o = jnp.einsum('pyshki,pshkj->yhij', left, right, preferred_element_type=F32)
    cols = o.shape[-1]
    o = jnp.moveaxis(o, 1, 0).reshape(per, col_count * cols, cols)
    mean_p = jnp.mean(o, axis=0)
    m2_p = jnp.sum((o - mean_p) ** 2, axis=0)
    mean = lax.pmean(mean_p, 'row')
    m2 = lax.psum(m2_p + per * (mean_p - mean) ** 2, 'row')
    g = lax.dynamic_slice_in_dim(gain, lax.axis_index('row') * per, per).astype(F32)
    y = ((o - mean) * lax.rsqrt(m2 / heads + LN_EPS) * g[:, None, None]).astype(BF16)
    y = jnp.transpose(y.reshape(per, row_count, 2 * half // 32, 32, cols), (1, 2, 3, 0, 4))
    wide = y[..., :LANES]
    narrow = jnp.concatenate([y[:, :, :16, :, LANES:], y[:, :, 16:, :, LANES:]], axis=-1)
    packed = jnp.concatenate([wide, narrow], axis=2)
    return lax.all_to_all(packed, 'row', 0, 0, tiled=True)


def solution(mesh):
    row_count = mesh.shape['row']
    col_count = mesh.shape['col']
    tile_spec = P(('batch', 'row'), 'col', None)
    mask_spec = P(('batch', 'row'), 'col')

    def local_step(z, mask, g_in, w_a, w_ag, w_b, w_bg, w_g, g_out, w_o):
        weights = jnp.concatenate([w_a, w_ag, w_b, w_bg], axis=1).T
        x, a, b = project(z, mask, g_in, weights)
        y = exchange(a, b, g_out, row_count, col_count)
        return finish(y, x, z, w_g, w_o)

    return jax.shard_map(local_step, mesh=mesh, in_specs=(tile_spec, mask_spec) + (P(),) * 8, out_specs=tile_spec, check_vma=False)
```

time: 668 us -> 527 us (0.79)
  waiting for transfers between devices: 315 us -> 197 us
  local copies, waits for them, and re-layouts: 113 us -> 49.3 us
  blocking collectives: 117 us -> 176 us
  Pallas kernels: 0 us -> 52.4 us
  matrix products: 60 us -> 13.8 us
  other arithmetic: 43.7 us -> 20.7 us
    all_gather x2 -> x1, waiting for transfers between devices: 314 us -> 111 us  [exchange(): all_a = lax.all_gather(got_a, 'col', axis=0)]
    reshape x2 -> x0, local copies, waits for them, and re-layouts: 96.9 us -> none  [the longest x1 67.3 us: local_step(): lax.all_gather(right_act, 'row', axis=0, tiled=True)]
    psum x0 -> x2, waiting for transfers between devices: none -> 86.4 us  [the longest x1 46.8 us: exchange(): mean = lax.pmean(mean_p, 'row')]
    all_to_all x2 -> x3, blocking collectives: 117 us -> 176 us  [the longest x1 59.4 us: exchange(): return lax.all_to_all(packed, 'row', 0, 0, tiled=True)]
    pallas_call x0 -> x2, Pallas kernels: none -> 52.4 us  [the longest x1 34.1 us: project(): pl.pallas_call(project_kernel, grid=(steps,), in_specs=[tile_spec, pl.Blo...]
    dot_general x3 -> x1, matrix products: 60 us -> 13.8 us  [exchange(): jnp.einsum('pyshki,pshkj->yhij', left, right, preferred_element_type=F32)]
    convert_element_type x5 -> x1, other arithmetic: 25.4 us -> 0.08 us  [exchange(): lax.dynamic_slice_in_dim(gain, lax.axis_index('row') * per, per).astype(F32)]
    dot_general x0 -> x1, local copies, waits for them, and re-layouts: none -> 16.3 us  [exchange(): jnp.einsum('pyshki,pshkj->yhij', left, right, preferred_element_type=F32)]
  transfers between devices with their start and end apart: 2 -> 3, of which waited for: 2 -> 3; matrix products, arithmetic and copies ran while one was open for 4% -> 5% of each run, Pallas kernels for 0% -> 0%
where the time goes in v1:
time: 527 us; the launch traced here: 523 us
  waiting for transfers between devices  197 us (37%)
  blocking collectives  176 us (33%)
  Pallas kernels  52.4 us (10%)
  local copies, waits for them, and re-layouts  49.3 us (9%)
  other arithmetic  20.7 us (4%)
  matrix products  13.8 us (3%)
  between operations  13.3 us (3%)
    all_gather x1, waiting for transfers between devices, exchange(): all_a = lax.all_gather(got_a, 'col', axis=0)  111 us
    all_to_all x1, blocking collectives, exchange(): return lax.all_to_all(packed, 'row', 0, 0, tiled=True)  59.4 us
    all_to_all x1, blocking collectives, exchange(): got_b = lax.all_to_all(b.reshape(wire), 'row', 0, 0, tiled=True)  58.9 us
    all_to_all x1, blocking collectives, exchange(): got_a = lax.all_to_all(a.reshape(wire), 'row', 0, 0, tiled=True)  57.2 us
    psum x1, waiting for transfers between devices, exchange(): mean = lax.pmean(mean_p, 'row')  46.8 us
    psum x1, waiting for transfers between devices, exchange(): m2 = lax.psum(m2_p + per * (mean_p - mean) ** 2, 'row')  39.6 us
    pallas_call x1, Pallas kernels, project(): pl.pallas_call(project_kernel, grid=(steps,), in_specs=[tile_spec, pl.Blo...  34.1 us
    pallas_call x1, Pallas kernels, finish(): pl.pallas_call(finish_kernel, grid=(groups,), in_specs=[pl.BlockSpec((src...  18.4 us
  transfers between devices with their start and end apart: 3, of which 3 were waited for; matrix products, arithmetic and copies ran while one was open for 5% of the time, Pallas kernels for 0%

profile of v1, /device:TPU:101, one launch (start us, length us, event | category | flops | bytes accessed | tf_op | source)
XLA Modules:
  0.0 522.6 jit_solution(8836416866590099188)
XLA Ops:
  6.5 0.0 all-gather.3.cloned.1.call-start
  6.6 0.8 slice_bitcast_fusion.1
  7.3 0.8 fusion.18
  8.1 0.9 copy.33
  8.9 0.9 copy.32
  9.8 0.9 copy.31
  10.7 0.9 copy.30
  11.6 0.1 pad_add_fusion.1
  11.6 0.1 pad_add_fusion
  11.7 0.7 pad.4
  12.4 0.7 maximum_bitcast_fusion.4.w_ref
  13.1 34.1 %shard_map.100 = (bf16[2,48,192,128]{3,2,1,0:T(8,128)(2,1)}, bf16[128,3,48,128]{3,2,1,0:T(8,128)(2,1)}, bf16[128,3,48,128]{3,2,1,0:T(8,128)(2,1)}) custom-call(bf16[2,48,192,128]{3,2,1,0:T(8,128)(2,1)} %bitcast.58, s32[3,16,8,128]{3,2,1,0:T(8,128)} %bitcast.62, bf16[1,128]{1,0:T(2,128)(2,1)} %bitcast.68, bf16[512,128]{1,0:T(8,128)(2,1)} %maximum_bitcast_fusion.4.w_ref), custom_call_target="tpu_custom_call" | custom-call | flops 2415919104 | bytes 18874368 | tf_op jit(solution)/shard_map/pallas_call | solution.py:73
  47.1 57.2 %all_to_all.15 = bf16[8,16,3,48,128]{4,3,2,1,0:T(8,128)(2,1)} all-to-all(bf16[8,16,3,48,128]{4,3,2,1,0:T(8,128)(2,1)} %bitcast.57), channel_id=1, replica_groups=mesh['batch'=1,'col'=4,'row'=8] {'row'}, dimensions={0} | all-to-all | bytes 9437184 | tf_op jit(solution)/shard_map/all_to_all | solution.py:142
  104.4 0.1 all-gather.3.cloned.1.call-update
  104.4 0.1 all-reduce.4.cloned.1.call-start
  104.5 58.9 %all_to_all.16 = bf16[8,16,3,48,128]{4,3,2,1,0:T(8,128)(2,1)S(1)} all-to-all(bf16[8,16,3,48,128]{4,3,2,1,0:T(8,128)(2,1)} %bitcast.56), channel_id=1, replica_groups=mesh['batch'=1,'col'=4,'row'=8] {'row'}, dimensions={0} | all-to-all | bytes 9437184 | tf_op jit(solution)/shard_map/all_to_all | solution.py:144
  163.4 1.4 copy.42
  164.8 0.5 slice.59
  165.3 2.3 fusion.17
  167.6 110.7 %all-gather.3.cloned.1.call-done = bf16[32,16,3,48,128]{4,3,2,1,0:T(8,128)(2,1)} async-done(((bf16[8,16,3,48,128]{4,3,2,1,0:T(8,128)(2,1)}), bf16[32,16,3,48,128]{4,3,2,1,0:T(8,128)(2,1)}) %all-gather.3.cloned.1.call-update) | async-done | bytes 18874384 | tf_op jit(solution)/shard_map/all_gather | solution.py:143
  278.3 11.4 %copy.41 = bf16[4,8,16,3,48,128]{5,4,1,3,0,2:T(8,128)(2,1)S(1)} copy(bf16[4,8,16,3,48,128]{5,4,3,2,1,0:T(8,128)(2,1)} %bitcast.54) | data formatting | bytes 37748736 | tf_op jit(solution)/shard_map/all_gather | solution.py:143
  289.8 6.5 %fusion.15 = (bf16[1,4,8,16,48,64]{5,4,2,0,1,3:T(8,128)(2,1)}, bf16[1,4,8,16,48,64]{5,4,2,0,1,3:T(8,128)(2,1)}) fusion(bf16[3,4,8,16,48,128]{5,4,2,0,1,3:T(8,128)(2,1)S(1)} %bitcast.49), kind=kLoop, calls=%fused_computation.29 | loop fusion | bytes 12582912 | tf_op jit(solution)/shard_map/slice | solution.py:148
  296.2 4.0 slice.56
  300.3 13.8 %fusion.19 = (f32[4,192,192]{2,1,0:T(8,128)S(1)}, f32[16,4,192,192]{3,2,1,0:T(8,128)}) fusion(bf16[1,8,16,48,64]{4,3,1,0,2:T(8,128)(2,1)} %get-tuple-element.16, bf16[1,8,16,48,64]{4,3,1,0,2:T(8,128)(2,1)} %get-tuple-element.15, bf16[2,8,16,48,128]{4,3,1,0,2:T(8,128)(2,1)S(1)} %slice.59, bf16[1,4,8,16,48,64]{5,4,2,0,1,3:T(8,128)(2,1)} %get-tuple-element.12, ...), kind=kOutput, calls=%fused_computation.33 | convolution fusion | flops 3696869376 | bytes 33619968 | tf_op jit(solution)/shard_map/pyshki,pshkj->yhij/dot_general | solution.py:152
  314.0 1.0 broadcast_multiply_fusion.1
  315.0 0.1 all-reduce.4.cloned.1.call-update
  315.1 0.2 all-reduce.6.cloned.1.call-start
  315.3 0.0 copy-start
  315.3 0.0 copy-start.1
  315.3 6.5 %multiply_reduce_fusion = f32[4,192,192]{2,1,0:T(8,128)S(1)} fusion(f32[16,4,192,192]{3,2,1,0:T(8,128)} %get-tuple-element.24, f32[4,192,192]{2,1,0:T(8,128)} %broadcast_multiply_fusion.1), kind=kLoop, calls=%fused_computation.8 | loop fusion | flops 6930432 | bytes 10616832 | tf_op jit(solution)/shard_map/reduce_sum | solution.py:156
  321.8 46.8 %all-reduce.4.cloned.1.call-done = f32[768,192]{1,0:T(8,128)} async-done(((f32[768,192]{1,0:T(8,128)}), f32[768,192]{1,0:T(8,128)}) %all-reduce.4.cloned.1.call-update) | async-done | bytes 589840 | tf_op jit(solution)/shard_map/psum | solution.py:157
  368.7 0.0 copy-done
  368.7 2.2 broadcast_multiply_fusion
  370.8 0.1 all-reduce.6.cloned.1.call-update
  370.9 0.0 copy-done.1
  370.9 0.1 dynamic-slice_convert_fusion
  371.0 16.3 %copy.36 = f32[16,4,192,192]{3,0,2,1:T(8,128)} copy(f32[16,4,192,192]{3,2,1,0:T(8,128)} %get-tuple-element.24) | data formatting | bytes 18874368 | tf_op jit(solution)/shard_map/pyshki,pshkj->yhij/dot_general | solution.py:152
  387.3 39.6 %all-reduce.6.cloned.1.call-done = f32[768,192]{1,0:T(8,128)} async-done(((f32[768,192]{1,0:T(8,128)}), f32[768,192]{1,0:T(8,128)}) %all-reduce.6.cloned.1.call-update) | async-done | bytes 589840 | tf_op jit(solution)/shard_map/psum | solution.py:158
  426.9 1.2 add_rsqrt_fusion
  428.2 6.9 %fusion.6 = bf16[8,3,32,16,192]{4,3,2,1,0:T(8,128)(2,1)S(1)} fusion(f32[16,8,3,32,192]{4,0,3,2,1:T(8,128)} %bitcast.51, f32[16]{0:T(128)S(1)} %dynamic-slice_convert_fusion, f32[8,3,32,192]{3,2,1,0:T(8,128)S(1)} %bitcast.60, f32[8,3,32,192]{3,2,1,0:T(8,128)S(1)} %bitcast.61), kind=kLoop, calls=%fused_computation.9 | loop fusion | flops 9437184 | bytes 15335488 | tf_op jit(solution)/shard_map/transpose | solution.py:161
  435.0 0.6 fusion.16
  435.6 0.6 slice.62
  436.2 2.1 maximum_maximum_fusion
  438.3 59.4 %all_to_all.17.y_ref = bf16[8,3,48,16,128]{4,3,2,1,0:T(8,128)(2,1)} all-to-all(bf16[8,3,48,16,128]{4,3,2,1,0:T(8,128)(2,1)S(1)} %maximum_maximum_fusion), channel_id=1, replica_groups=mesh['batch'=1,'col'=4,'row'=8] {'row'}, dimensions={0} | all-to-all | bytes 9437184 | tf_op jit(solution)/shard_map/all_to_all | solution.py:165
  497.6 18.4 %shard_map.101 = bf16[96,192,128]{2,1,0:T(8,128)(2,1)} custom-call(bf16[8,3,48,16,128]{4,3,2,1,0:T(8,128)(2,1)} %all_to_all.17.y_ref, bf16[96,192,128]{2,1,0:T(8,128)(2,1)} %bitcast.59, bf16[96,192,128]{2,1,0:T(8,128)(2,1)} %z_ref.1, bf16[128,128]{1,0:T(8,128)(2,1)} %wg_ref.1, bf16[128,128]{1,0:T(8,128)(2,1)} %wo_ref.1), custom_call_target="tpu_custom_call" | custom-call | flops 1207959552 | bytes 18874368 | tf_op jit(solution)/shard_map/pallas_call | solution.py:121
Async XLA Ops:
  6.5 271.8 %all-gather.3.cloned.1.call-start = ((), (), s32[]{:S(2)}) async-start(), calls=%async_computation.5 | async-start | bytes 23592960 | tf_op jit(solution)/shard_map/all_gather | solution.py:143
  104.4 264.2 %all-reduce.4.cloned.1.call-start = ((), (), s32[]{:S(2)}) async-start(), calls=%async_computation.3 | async-start | bytes 1572864 | tf_op jit(solution)/shard_map/psum | solution.py:157
  315.1 111.8 %all-reduce.6.cloned.1.call-start = ((), (), s32[]{:S(2)}) async-start(), calls=%async_computation.4 | async-start | bytes 1572864 | tf_op jit(solution)/shard_map/psum | solution.py:158
  315.3 53.3 %copy-start = (f32[4,192,192]{2,1,0:T(8,128)S(1)}, f32[4,192,192]{2,1,0:T(8,128)}, u32[]{:S(2)}) copy-start(f32[4,192,192]{2,1,0:T(8,128)} %broadcast_multiply_fusion.1) | copy-start | bytes 1769476
  315.3 55.6 %copy-start.1 = (bf16[128]{0:T(256)(128)(2,1)S(1)}, bf16[128]{0:T(256)(128)(2,1)}, u32[]{:S(2)}) copy-start(bf16[128]{0:T(256)(128)(2,1)} %param.18) | copy-start | bytes 772
Sparse Core Ops, SparseCore 0:
  104.5 173.7 all-gather.2
  315.2 53.4 all-reduce.3
  371.0 55.8 all-reduce.5

commit v2 on v1

--- a/solution.py
+++ b/solution.py
@@ -135,34 +135,301 @@
     )(y, x.reshape(z.shape), z, w_gate, w_out)
 
 
+def remote(src, dst, send_sem, recv_sem, **place):
+    return pltpu.make_async_remote_copy(
+        src_ref=src, dst_ref=dst, send_sem=send_sem, recv_sem=recv_sem, device_id=place, device_id_type=pl.DeviceIdType.MESH
+    )
+
+
+def exchange_kernel(
+    row_count, col_count, a_hbm, b_hbm, g_ref, y_hbm, all_a, got_b, rhs, o_wide, o_tail, st_part, st_got, st_tot, y_out,
+    xa_s, xa_r, xb_s, xb_r, dir_s, dir_r, fwd_s, fwd_r, rs_s, rs_r, ag_s, ag_r, ys_s, ys_r, loc,
+):
+    me, col = lax.axis_index('row'), lax.axis_index('col')
+    per, _, half, _ = a_hbm.shape[1:]
+    heads = per * row_count
+    depth = row_count * half
+    cols = LANES + HALF
+    chip, core = me // 2, me % 2
+    chips = row_count // 2
+    steps = [(0, 0), (0, 1)]
+    for d in range(1, chips // 2 + 1):
+        steps += [(d, 0), (-d, 0), (d, 1), (-d, 1)] if 2 * d < chips else [(d, 0), (d, 1)]
+    peers = [lax.rem(chip + d + chips, chips) * 2 + lax.rem(core + f, 2) for d, f in steps]
+    up, down = lax.rem(col + 1, col_count), lax.rem(col + col_count - 1, col_count)
+    far = lax.rem(col + 2, col_count)
+
+    barrier = pltpu.get_barrier_semaphore()
+    for p in peers[1:]:
+        pl.semaphore_signal(barrier, inc=1, device_id={'row': p}, device_id_type=pl.DeviceIdType.MESH)
+    for p in (up, down):
+        pl.semaphore_signal(barrier, inc=1, device_id={'col': p}, device_id_type=pl.DeviceIdType.MESH)
+    pl.semaphore_wait(barrier, row_count + 1)
+
+    own_a = pltpu.make_async_copy(a_hbm.at[me], all_a.at[col, me], loc.at[0])
+    own_b = pltpu.make_async_copy(b_hbm.at[me], got_b.at[me], loc.at[1])
+    sends = []
+
+    def send(*args, **place):
+        copy = remote(*args, **place)
+        copy.start()
+        sends.append(copy)
+
+    def direct(q):
+        src = all_a.at[col, peers[q]]
+        send(src, src, dir_s.at[0, q], dir_r.at[0, peers[q]], col=up)
+        send(src, src, dir_s.at[1, q], dir_r.at[1, peers[q]], col=down)
+
+    own_a.start()
+    for q in range(1, row_count):
+        send(a_hbm.at[peers[q]], all_a.at[col, me], xa_s.at[q], xa_r.at[me], row=peers[q])
+    own_b.start()
+    for q in range(1, row_count):
+        send(b_hbm.at[peers[q]], got_b.at[me], xb_s.at[q], xb_r.at[me], row=peers[q])
+
+    own_a.wait()
+    direct(0)
+    for q in range(1, row_count):
+        remote(a_hbm.at[me], all_a.at[col, peers[q]], xa_s.at[q], xa_r.at[peers[q]], row=peers[q]).wait_recv()
+        direct(q)
+
+    def forward(q, part):
+        away, block = (up, down) if q % 2 == 0 else (down, up)
+        src = all_a.at[block, peers[q], :, pl.ds(2 * part, 2 - part)]
+        send(src, src, fwd_s.at[part, q], fwd_r.at[part, peers[q]], col=away)
+
+    for q in range(row_count):
+        for way, block in ((0, down), (1, up)):
+            ref = all_a.at[block, peers[q]]
+            remote(ref, ref, dir_s.at[way, q], dir_r.at[way, peers[q]], col=up).wait_recv()
+        forward(q, 0)
+    for q in range(row_count):
+        forward(q, 1)
+
+    own_b.wait()
+    for q in range(1, row_count):
+        remote(b_hbm.at[me], got_b.at[peers[q]], xb_s.at[q], xb_r.at[peers[q]], row=peers[q]).wait_recv()
+
+    def spread(h, carry):
+        tail = got_b[:, h, 2].reshape(depth, LANES)
+        for s in range(2):
+            rhs[h, s, :, :LANES] = got_b[:, h, s].reshape(depth, LANES)
+        rhs[h, 0, :, LANES:] = tail
+        rhs[h, 1, :, LANES:] = jnp.concatenate([tail[:, HALF:], tail[:, :HALF]], axis=1)
+        return carry
+
+    lax.fori_loop(0, per, spread, 0)
+
+    lane = lax.broadcasted_iota(jnp.int32, (8, LANES), 1)
+    pitch = o_wide.shape[2]
+    flat_wide = o_wide.reshape(col_count * per * pitch, LANES)
+    flat_tail = o_tail.reshape(col_count * per * pitch, LANES)
+
+    def swap(v):
+        return pltpu.roll(v, HALF, v.ndim - 1)
+
+    def product(block, row0, rows):
+        def channel(h, carry):
+            if row0 == 0:
+                res = dot(all_a[block, :, h, 0].reshape(depth, LANES), rhs[h, 0], ((0,), (0,)))
+                res += dot(all_a[block, :, h, 1].reshape(depth, LANES), rhs[h, 1], ((0,), (0,)))
+                o_wide[block, h, 0:LANES] = res[:, :LANES]
+                o_tail[block, h, 0:LANES] = res[:, LANES:]
+            if row0 + rows == cols:
+                turned = all_a[block, :, h, 2].reshape(depth, LANES).T
+                res = dot(turned[:HALF], rhs[h, 0], ((1,), (0,)))
+                res += dot(turned[HALF:], rhs[h, 1], ((1,), (0,)))
+                o_wide[block, h, LANES:cols] = res[:, :LANES]
+                o_tail[block, h, LANES:cols] = res[:, LANES:]
+            return carry
+
+        lax.fori_loop(0, per, channel, 0)
+
+    def partial(u, block, row0, rows):
+        def tile(t, carry):
+            at = pl.ds(pl.multiple_of(row0 + 8 * t, 8), 8)
+            out = []
+            for ref in (o_wide, o_tail):
+                v = ref[block, :, at]
+                mean = jnp.sum(v, axis=0) * (1.0 / per)
+                out += [mean, jnp.sum((v - mean) ** 2, axis=0)]
+            st_part[block, 0, at] = out[0]
+            st_part[block, 1, at] = out[1]
+            st_part[block, 2, at] = jnp.where(lane < HALF, out[2], swap(out[3]))
+            return carry
+
+        lax.fori_loop(0, rows // 8, tile, 0)
+        own = rows // row_count
+        for q in range(1, row_count):
+            at = pl.ds(pl.multiple_of(row0 + own * peers[q], 8), own)
+            send(st_part.at[block, :, at], st_got.at[u, me, :, 0:own], rs_s.at[u, q], rs_r.at[u, me], row=peers[q])
+
+    def combine(u, block, row0, rows):
+        own = rows // row_count
+        first = pl.multiple_of(row0 + own * me, 8)
+        st_got[u, me, :, 0:own] = st_part[block, :, pl.ds(first, own)]
+        for q in range(1, row_count):
+            ref = st_got.at[u, peers[q], :, 0:own]
+            remote(ref, ref, rs_s.at[u, q], rs_r.at[u, peers[q]], row=peers[q]).wait_recv()
+        for t in range(own // 8):
+            at = slice(8 * t, 8 * t + 8)
+            to = pl.ds(pl.multiple_of(first + 8 * t, 8), 8)
+            means, squares, both = st_got[u, :, 0, at], st_got[u, :, 1, at], st_got[u, :, 2, at]
+            mean = jnp.sum(means, axis=0) * (1.0 / row_count)
+            square = jnp.sum(squares, axis=0) + per * jnp.sum((means - mean) ** 2, axis=0)
+            st_tot[block, 0, to] = mean
+            st_tot[block, 1, to] = lax.rsqrt(square * (1.0 / heads) + LN_EPS)
+            total = jnp.sum(both, axis=0)
+            mean = total * (1.0 / row_count)
+            square = total + swap(per * jnp.sum((both - mean) ** 2, axis=0))
+            st_tot[block, 2, to] = jnp.where(lane < HALF, mean, lax.rsqrt(square * (1.0 / heads) + LN_EPS))
+        for q in range(1, row_count):
+            ref = st_tot.at[block, :, pl.ds(first, own)]
+            send(ref, ref, ag_s.at[u, q], ag_r.at[u, me], row=peers[q])
+
+    gain = g_ref[pl.ds(pl.multiple_of(me * per, 8), per), :]
+    wide_lane = lax.broadcasted_iota(jnp.int32, (per, LANES), 1)
+
+    def normalize(u, block, row0, rows):
+        own = rows // row_count
+        for q in range(1, row_count):
+            ref = st_tot.at[block, :, pl.ds(pl.multiple_of(row0 + own * peers[q], 8), own)]
+            remote(ref, ref, ag_s.at[u, q], ag_r.at[u, peers[q]], row=peers[q]).wait_recv()
+        base = block * (per * pitch)
+
+        def wide(t, carry):
+            for s in range(8):
+                i = row0 + 8 * t + s
+                v = flat_wide[pl.ds(base + i, per, stride=pitch), :]
+                v = (v - st_tot[block, 0, pl.ds(i, 1)]) * st_tot[block, 1, pl.ds(i, 1)] * gain
+                y_out[block, i // 32, i % 32] = v.astype(BF16)
+            return carry
+
+        def tail(t, carry):
+            for s in range(8):
+                i = row0 + 32 * (t // 2) + 8 * (t % 2) + s
+                lo = flat_tail[pl.ds(base + i, per, stride=pitch), :]
+                hi = flat_tail[pl.ds(base + i + 16, per, stride=pitch), :]
+                first, second = st_tot[block, 2, pl.ds(i, 1)], st_tot[block, 2, pl.ds(i + 16, 1)]
+                v = jnp.where(wide_lane < HALF, lo, swap(hi))
+                mean = jnp.where(wide_lane[:1] < HALF, first, swap(second))
+                rstd = jnp.where(wide_lane[:1] < HALF, swap(first), second)
+                y_out[block, i // 32, 32 + i % 32] = ((v - mean) * rstd * gain).astype(BF16)
+            return carry
+
+        lax.fori_loop(0, rows // 8, wide, 0)
+        lax.fori_loop(0, rows // 16, tail, 0)
+
+    def back(block, slot, pieces):
+        for c, p in pieces:
+            dest = block * 2 + c
+            src = y_out.at[block, pl.ds(3 * c + p, 1 + p)]
+            dst = y_hbm.at[me, pl.ds(p, 1 + p)]
+
+            @pl.when(dest != me)
+            def _():
+                remote(src, dst, ys_s.at[slot, c, p], ys_r.at[me, p], row=dest).start()
+
+            @pl.when(dest == me)
+            def _():
+                pltpu.make_async_copy(src, dst, loc.at[2 + p]).start()
+
+    def back_done(block, slot):
+        for c in range(2):
+            for p in range(2):
+                dest = block * 2 + c
+                src = y_out.at[block, pl.ds(3 * c + p, 1 + p)]
+                dst = y_hbm.at[me, pl.ds(p, 1 + p)]
+
+                @pl.when(dest != me)
+                def _():
+                    remote(src, dst, ys_s.at[slot, c, p], ys_r.at[me, p], row=dest).wait_send()
+
+                @pl.when(dest == me)
+                def _():
+                    pltpu.make_async_copy(src, dst, loc.at[2 + p]).wait()
+
+    def arrived(part):
+        for q in range(row_count):
+            block = far
+            ref = all_a.at[block, peers[q], :, pl.ds(2 * part, 2 - part)]
+            remote(ref, ref, fwd_s.at[part, q], fwd_r.at[part, peers[q]], col=up).wait_recv()
+
+    wide_rows, all_rows = (0, LANES), (0, cols)
+    every = ((0, 0), (0, 1), (1, 0), (1, 1))
+    units = [(0, col) + all_rows, (1, down) + all_rows, (2, up) + all_rows, (3, far) + wide_rows, (4, far, LANES, HALF)]
+
+    def start(u):
+        product(*units[u][1:])
+        partial(*units[u])
+
+    start(0)
+    start(1)
+    combine(*units[0])
+    start(2)
+    combine(*units[1])
+    normalize(*units[0])
+    back(col, 0, every)
+    combine(*units[2])
+    normalize(*units[1])
+    back(down, 1, every)
+    normalize(*units[2])
+    back(up, 2, every)
+    arrived(0)
+    start(3)
+    combine(*units[3])
+    arrived(1)
+    start(4)
+    normalize(*units[3])
+    back(far, 3, ((0, 0), (0, 1), (1, 0)))
+    combine(*units[4])
+    normalize(*units[4])
+    back(far, 3, ((1, 1),))
+
+    for copy in sends:
+        copy.wait_send()
+    for slot, block in enumerate((col, down, up, far)):
+        back_done(block, slot)
+    for q in range(1, row_count):
+        for p in range(2):
+            ref = y_hbm.at[peers[q], pl.ds(p, 1 + p)]
+            remote(y_out.at[0, pl.ds(p, 1 + p)], ref, ys_s.at[0, 0, p], ys_r.at[peers[q], p], row=peers[q]).wait_recv()
+
+
 def exchange(a, b, gain, row_count, col_count):
     heads, _, half, _ = a.shape
     per = heads // row_count
+    cols = 2 * half * row_count // col_count
+    depth = row_count * half
+    groups = 2 * half // 32
     wire = (row_count, per, 3, half, LANES)
-    got_a = lax.all_to_all(a.reshape(wire), 'row', 0, 0, tiled=True)
-    all_a = lax.all_gather(got_a, 'col', axis=0)
-    got_b = lax.all_to_all(b.reshape(wire), 'row', 0, 0, tiled=True)
-
-    def unpack(w):
-        w = jnp.moveaxis(w, -3, 0)
-        tail = jnp.stack([w[2, ..., :HALF], w[2, ..., HALF:]])
-        return jnp.concatenate([w[:2], tail], axis=-1)
-
-    left, right = unpack(all_a), unpack(got_b)
-    o = jnp.einsum('pyshki,pshkj->yhij', left, right, preferred_element_type=F32)
-    cols = o.shape[-1]
-    o = jnp.moveaxis(o, 1, 0).reshape(per, col_count * cols, cols)
-    mean_p = jnp.mean(o, axis=0)
-    m2_p = jnp.sum((o - mean_p) ** 2, axis=0)
-    mean = lax.pmean(mean_p, 'row')
-    m2 = lax.psum(m2_p + per * (mean_p - mean) ** 2, 'row')
-    g = lax.dynamic_slice_in_dim(gain, lax.axis_index('row') * per, per).astype(F32)
-    y = ((o - mean) * lax.rsqrt(m2 / heads + LN_EPS) * g[:, None, None]).astype(BF16)
-    y = jnp.transpose(y.reshape(per, row_count, 2 * half // 32, 32, cols), (1, 2, 3, 0, 4))
-    wide = y[..., :LANES]
-    narrow = jnp.concatenate([y[:, :, :16, :, LANES:], y[:, :, 16:, :, LANES:]], axis=-1)
-    packed = jnp.concatenate([wide, narrow], axis=2)
-    return lax.all_to_all(packed, 'row', 0, 0, tiled=True)
+    dma = pltpu.SemaphoreType.DMA
+    pitch = cols + 8
+    gains = jnp.broadcast_to(gain.astype(F32)[:, None], (heads, LANES))
+    hbm = pl.BlockSpec(memory_space=pl.ANY)
+    return pl.pallas_call(
+        functools.partial(exchange_kernel, row_count, col_count),
+        in_specs=[hbm, hbm, pl.BlockSpec(memory_space=pltpu.VMEM)],
+        out_specs=hbm,
+        out_shape=jax.ShapeDtypeStruct((row_count, groups, 48, per, LANES), BF16),
+        scratch_shapes=[
+            pltpu.VMEM((col_count,) + wire, BF16),
+            pltpu.VMEM(wire, BF16),
+            pltpu.VMEM((per, 2, depth, 2 * LANES), BF16),
+            pltpu.VMEM((col_count, per, pitch, LANES), F32),
+            pltpu.VMEM((col_count, per, pitch, LANES), F32),
+            pltpu.VMEM((col_count, 3, cols, LANES), F32),
+            pltpu.VMEM((5, row_count, 3, cols // row_count, LANES), F32),
+            pltpu.VMEM((col_count, 3, cols, LANES), F32),
+            pltpu.VMEM((col_count, 2 * groups, 48, per, LANES), BF16),
+            dma((row_count,)), dma((row_count,)), dma((row_count,)), dma((row_count,)),
+            dma((2, row_count)), dma((2, row_count)), dma((2, row_count)), dma((2, row_count)),
+            dma((5, row_count)), dma((5, row_count)), dma((5, row_count)), dma((5, row_count)),
+            dma((col_count, 2, 2)), dma((row_count, 2)), dma((4,)),
+        ],
+        compiler_params=pltpu.CompilerParams(collective_id=0, has_side_effects=True, vmem_limit_bytes=62 * 2**20),
+        cost_estimate=pl.CostEstimate(flops=2 * per * depth * 2 * cols * col_count * cols, bytes_accessed=a.size * 8, transcendentals=0),
+    )(a.reshape(wire), b.reshape(wire), gains)
 
 
 def solution(mesh):

time: 527 us -> 353 us (0.67)
  Pallas kernels: 52.4 us -> 345 us
  waiting for transfers between devices: 197 us -> 0 us
  blocking collectives: 176 us -> 0 us
  local copies, waits for them, and re-layouts: 49.3 us -> 7.06 us
  other arithmetic: 20.7 us -> 0.81 us
  matrix products: 13.8 us -> 0 us
  between operations: 13.3 us -> 0.04 us
    pallas_call x0 -> x1, Pallas kernels: none -> 293 us  [exchange(): pl.pallas_call(functools.partial(exchange_kernel, row_count, col_count),...]
    all_to_all x3 -> x0, blocking collectives: 176 us -> none  [the longest x1 59.4 us: exchange(): return lax.all_to_all(packed, 'row', 0, 0, tiled=True)]
    all_gather x1 -> x0, waiting for transfers between devices: 111 us -> none  [exchange(): all_a = lax.all_gather(got_a, 'col', axis=0)]
    psum x2 -> x0, waiting for transfers between devices: 86.4 us -> none  [the longest x1 46.8 us: exchange(): mean = lax.pmean(mean_p, 'row')]
    dot_general x1 -> x0, local copies, waits for them, and re-layouts: 16.3 us -> none  [exchange(): jnp.einsum('pyshki,pshkj->yhij', left, right, preferred_element_type=F32)]
    slice x6 -> x0, local copies, waits for them, and re-layouts: 14.5 us -> none  [the longest x2 8.81 us: unpack(): tail = jnp.stack([w[2, ..., :HALF], w[2, ..., HALF:]])]
    dot_general x1 -> x0, matrix products: 13.8 us -> none  [exchange(): jnp.einsum('pyshki,pshkj->yhij', left, right, preferred_element_type=F32)]
    all_gather x1 -> x0, local copies, waits for them, and re-layouts: 11.4 us -> none  [exchange(): all_a = lax.all_gather(got_a, 'col', axis=0)]
  transfers between devices with their start and end apart: 3 -> 0, of which waited for: 3 -> 0; matrix products, arithmetic and copies ran while one was open for 5% -> 0% of each run, Pallas kernels for 0% -> 0%
where the time goes in v2:
time: 353 us
  Pallas kernels  345 us (98%)
  local copies, waits for them, and re-layouts  7.06 us (2%)
    pallas_call x1, Pallas kernels, exchange(): pl.pallas_call(functools.partial(exchange_kernel, row_count, col_count),...  293 us
    pallas_call x1, Pallas kernels, project(): pl.pallas_call(project_kernel, grid=(steps,), in_specs=[tile_spec, pl.Blo...  34.1 us
    pallas_call x1, Pallas kernels, finish(): pl.pallas_call(finish_kernel, grid=(groups,), in_specs=[pl.BlockSpec((src...  18.4 us

profile of v2, /device:TPU:101, one launch (start us, length us, event | category | flops | bytes accessed | tf_op | source)
XLA Modules:
  0.0 352.9 jit_solution(8308963815862977149)
XLA Ops:
  0.0 0.9 copy.13
  0.9 0.9 copy.14
  1.7 0.9 copy.15
  2.6 0.9 copy.16
  3.5 0.7 maximum_bitcast_fusion.w_ref
  4.2 0.8 slice_bitcast_fusion.1
  4.9 0.1 pad_add_fusion.1
  5.0 0.8 fusion
  5.8 0.1 pad_add_fusion
  5.8 1.4 broadcast_in_dim.2.g_ref
  7.2 0.7 pad.4
  7.9 34.1 %shard_map.100 = (bf16[2,48,192,128]{3,2,1,0:T(8,128)(2,1)}, bf16[128,3,48,128]{3,2,1,0:T(8,128)(2,1)}, bf16[128,3,48,128]{3,2,1,0:T(8,128)(2,1)}) custom-call(bf16[2,48,192,128]{3,2,1,0:T(8,128)(2,1)} %bitcast.22, s32[3,16,8,128]{3,2,1,0:T(8,128)} %bitcast.24, bf16[1,128]{1,0:T(2,128)(2,1)} %bitcast.30, bf16[512,128]{1,0:T(8,128)(2,1)} %maximum_bitcast_fusion.w_ref), custom_call_target="tpu_custom_call" | custom-call | flops 2415919104 | bytes 18874368 | tf_op jit(solution)/shard_map/pallas_call | solution.py:73
  42.0 292.5 %shard_map.101.y_ref = bf16[8,3,48,16,128]{4,3,2,1,0:T(8,128)(2,1)} custom-call(bf16[8,16,3,48,128]{4,3,2,1,0:T(8,128)(2,1)} %bitcast.20, bf16[8,16,3,48,128]{4,3,2,1,0:T(8,128)(2,1)} %bitcast.21, f32[128,128]{1,0:T(8,128)} %broadcast_in_dim.2.g_ref), custom_call_target="tpu_custom_call" | custom-call | flops 3623878656 | bytes 18874368 | tf_op jit(solution)/shard_map/pallas_call | solution.py:410
  334.5 18.4 %shard_map.102 = bf16[96,192,128]{2,1,0:T(8,128)(2,1)} custom-call(bf16[8,3,48,16,128]{4,3,2,1,0:T(8,128)(2,1)} %shard_map.101.y_ref, bf16[96,192,128]{2,1,0:T(8,128)(2,1)} %bitcast.23, bf16[96,192,128]{2,1,0:T(8,128)(2,1)} %z_ref.1, bf16[128,128]{1,0:T(8,128)(2,1)} %wg_ref.1, bf16[128,128]{1,0:T(8,128)(2,1)} %wo_ref.1), custom_call_target="tpu_custom_call" | custom-call | flops 1207959552 | bytes 18874368 | tf_op jit(solution)/shard_map/pallas_call | solution.py:121

commit v3 on v1

--- a/solution.py
+++ b/solution.py
@@ -37,13 +37,14 @@
         hi = layer_norm(z_ref[1, t].astype(F32), gain).astype(BF16)
         x_ref[0, t] = lo
         x_ref[1, t] = hi
-        parts = (lo[:LANES], hi[:LANES], jnp.concatenate([lo[LANES:], hi[LANES:]], axis=0))
-        mask = m_ref[0, t].astype(F32)
-        for seg in range(3):
-            keep = mask[seg:seg + 1]
-            for side in range(2):
-                both = dot(w_ref[2 * side * heads:2 * (side + 1) * heads], parts[seg], ((1,), (1,)))
-                act = keep * jax.nn.sigmoid(both[heads:]) * both[:heads]
+        parts = [v[HALF * s:HALF * (s + 1)] for s in range(3) for v in (lo, hi)]
+        tall = jnp.concatenate(parts, axis=0)
+        keep = m_ref[0, t].astype(F32)
+        for side in range(2):
+            both = dot(w_ref[2 * side * heads:2 * (side + 1) * heads], tall, ((1,), (1,)))
+            for seg in range(3):
+                at = slice(seg * LANES, (seg + 1) * LANES)
+                act = keep[seg:seg + 1] * jax.nn.sigmoid(both[heads:, at]) * both[:heads, at]
                 flat[pl.ds((2 * seg + side) * heads * PITCH + t, heads, stride=PITCH), :] = act
         return carry
 
@@ -63,9 +64,7 @@
     half = rows // 2
     heads = weights.shape[0] // 4
     steps = half // GROUP
-    m = mask.reshape(2, half, cols)
-    tail = jnp.concatenate([m[0, :, LANES:], m[1, :, LANES:]], axis=-1)
-    m = jnp.stack([m[0, :, :LANES], m[1, :, :LANES], tail], axis=1)
+    m = mask.reshape(2, half, 3, HALF).transpose(1, 2, 0, 3).reshape(half, 3, LANES)
     m = jnp.pad(m, ((0, 0), (0, 5), (0, 0))).reshape(steps, GROUP, 8, LANES)
     wire = jax.ShapeDtypeStruct((heads, 3, half, LANES), BF16)
     wire_spec = pl.BlockSpec((heads, 3, GROUP, LANES), lambda t: (0, 0, t, 0))
@@ -135,34 +134,287 @@
     )(y, x.reshape(z.shape), z, w_gate, w_out)
 
 
+def remote(src, dst, send_sem, recv_sem, **place):
+    return pltpu.make_async_remote_copy(
+        src_ref=src, dst_ref=dst, send_sem=send_sem, recv_sem=recv_sem, device_id=place, device_id_type=pl.DeviceIdType.MESH
+    )
+
+
+MESSAGES = (((0, 0, 2, 0, 0),), ((0, 2, 1, 2, 1), (1, 3, 1, 0, 0)), ((1, 4, 2, 1, 1),))
+ARRIVALS = (((0, 2), (2, 1)), ((0, 1), (1, 2)))
+
+
+def exchange_kernel(
+    row_count, col_count, a_hbm, b_hbm, g_ref, y_hbm, all_a, got_b, rhs, o_wide, o_tail, st_part, st_got, st_tot, y_out,
+    xa_s, xa_r, xb_s, xb_r, dir_s, dir_r, fwd_s, fwd_r, rs_s, rs_r, ag_s, ag_r, ys_s, ys_r, loc,
+):
+    me, col = lax.axis_index('row'), lax.axis_index('col')
+    per, _, half, _ = a_hbm.shape[1:]
+    heads = per * row_count
+    depth = row_count * half
+    chip, core = me // 2, me % 2
+    chips = row_count // 2
+    steps = [(0, 0), (0, 1)]
+    for d in range(1, chips // 2 + 1):
+        steps += [(d, 0), (-d, 0), (d, 1), (-d, 1)] if 2 * d < chips else [(d, 0), (d, 1)]
+    peers = [lax.rem(chip + d + chips, chips) * 2 + lax.rem(core + f, 2) for d, f in steps]
+    blocks = [lax.rem(chip + d, chips) for d in (1, 3, 2, 0)]
+    up, down = lax.rem(col + 1, col_count), lax.rem(col + col_count - 1, col_count)
+    far = lax.rem(col + 2, col_count)
+
+    barrier = pltpu.get_barrier_semaphore()
+    for p in peers[1:]:
+        pl.semaphore_signal(barrier, inc=1, device_id={'row': p}, device_id_type=pl.DeviceIdType.MESH)
+    for p in (up, down):
+        pl.semaphore_signal(barrier, inc=1, device_id={'col': p}, device_id_type=pl.DeviceIdType.MESH)
+    pl.semaphore_wait(barrier, row_count + 1)
+
+    sends = []
+
+    def send(*args, **place):
+        copy = remote(*args, **place)
+        copy.start()
+        sends.append(copy)
+
+    own_a = [pltpu.make_async_copy(a_hbm.at[me, :, s], all_a.at[s, col, me], loc.at[s]) for s in range(3)]
+    own_b = pltpu.make_async_copy(b_hbm.at[me], got_b.at[me], loc.at[3])
+
+    def scatter_a(s):
+        own_a[s].start()
+        for q in range(1, row_count):
+            send(a_hbm.at[peers[q], :, s], all_a.at[s, col, me], xa_s.at[s, q], xa_r.at[s, me], row=peers[q])
+
+    def scatter_b():
+        own_b.start()
+        for q in range(1, row_count):
+            send(b_hbm.at[peers[q]], got_b.at[me], xb_s.at[q], xb_r.at[me], row=peers[q])
+
+    def direct(s):
+        own_a[s].wait()
+        for q in range(row_count):
+            src = all_a.at[s, col, peers[q]]
+            if q:
+                remote(src, src, xa_s.at[s, q], xa_r.at[s, peers[q]], row=peers[q]).wait_recv()
+            send(src, src, dir_s.at[s, 0, q], dir_r.at[s, 0, peers[q]], col=up)
+            send(src, src, dir_s.at[s, 1, q], dir_r.at[s, 1, peers[q]], col=down)
+
+    def forward(s, first, last):
+        for q in range(first, last):
+            for way, block in ((0, down), (1, up)):
+                ref = all_a.at[s, block, peers[q]]
+                remote(ref, ref, dir_s.at[s, way, q], dir_r.at[s, way, peers[q]], col=up).wait_recv()
+            away, block = (up, down) if q % 2 == 0 else (down, up)
+            src = all_a.at[s, block, peers[q]]
+            send(src, src, fwd_s.at[s, q], fwd_r.at[s, peers[q]], col=away)
+
+    def arrived(s):
+        for q in range(row_count):
+            ref = all_a.at[s, far, peers[q]]
+            remote(ref, ref, fwd_s.at[s, q], fwd_r.at[s, peers[q]], col=up).wait_recv()
+
+    lane = lax.broadcasted_iota(jnp.int32, (8, LANES), 1)
+    pitch = o_wide.shape[2]
+    rows = col_count * HALF
+    own = rows // row_count
+    flat_wide = o_wide.reshape(3 * per * pitch, LANES)
+    flat_tail = o_tail.reshape(3 * per * pitch, LANES)
+
+    def swap(v):
+        return pltpu.roll(v, HALF, v.ndim - 1)
+
+    def spread():
+        own_b.wait()
+        for q in range(1, row_count):
+            ref = got_b.at[peers[q]]
+            remote(ref, ref, xb_s.at[q], xb_r.at[peers[q]], row=peers[q]).wait_recv()
+
+        def channel(h, carry):
+            w = [got_b[:, h, s].reshape(depth, LANES) for s in range(3)]
+            rhs[h, 0, :, :LANES] = jnp.concatenate([w[0][:, :HALF], w[1][:, :HALF]], axis=1)
+            rhs[h, 1, :, :LANES] = jnp.concatenate([w[0][:, HALF:], w[1][:, HALF:]], axis=1)
+            rhs[h, 0, :, LANES:] = w[2]
+            rhs[h, 1, :, LANES:] = jnp.concatenate([w[2][:, HALF:], w[2][:, :HALF]], axis=1)
+            return carry
+
+        lax.fori_loop(0, per, channel, 0)
+
+    def product(u):
+        def channel(h, carry):
+            turned = [all_a[u, c, :, h].reshape(depth, LANES).T for c in range(col_count)]
+            res = dot(jnp.concatenate([t[:HALF] for t in turned], axis=0), rhs[h, 0], ((1,), (0,)))
+            res += dot(jnp.concatenate([t[HALF:] for t in turned], axis=0), rhs[h, 1], ((1,), (0,)))
+            o_wide[u, h, 0:rows] = res[:, :LANES]
+            o_tail[u, h, 0:rows] = res[:, LANES:]
+            return carry
+
+        lax.fori_loop(0, per, channel, 0)
+
+    def partial(u):
+        def tile(t, carry):
+            at = pl.ds(pl.multiple_of(8 * t, 8), 8)
+            out = []
+            for ref in (o_wide, o_tail):
+                v = ref[u, :, at]
+                mean = jnp.sum(v, axis=0) * (1.0 / per)
+                out += [mean, jnp.sum((v - mean) ** 2, axis=0)]
+            st_part[u, 0, at] = out[0]
+            st_part[u, 1, at] = out[1]
+            st_part[u, 2, at] = jnp.where(lane < HALF, out[2], swap(out[3]))
+            return carry
+
+        lax.fori_loop(0, rows // 8, tile, 0, unroll=2)
+        for q in range(1, row_count):
+            at = pl.ds(pl.multiple_of(own * peers[q], 8), own)
+            send(st_part.at[u, :, at], st_got.at[u, me], rs_s.at[u, q], rs_r.at[u, me], row=peers[q])
+
+    def combine(u):
+        first = pl.multiple_of(own * me, 8)
+        st_got[u, me] = st_part[u, :, pl.ds(first, own)]
+        for q in range(1, row_count):
+            ref = st_got.at[u, peers[q]]
+            remote(ref, ref, rs_s.at[u, q], rs_r.at[u, peers[q]], row=peers[q]).wait_recv()
+        for t in range(own // 8):
+            at = slice(8 * t, 8 * t + 8)
+            to = pl.ds(pl.multiple_of(first + 8 * t, 8), 8)
+            means, squares, both = st_got[u, :, 0, at], st_got[u, :, 1, at], st_got[u, :, 2, at]
+            mean = jnp.sum(means, axis=0) * (1.0 / row_count)
+            square = jnp.sum(squares, axis=0) + per * jnp.sum((means - mean) ** 2, axis=0)
+            st_tot[u, 0, to] = mean
+            st_tot[u, 1, to] = lax.rsqrt(square * (1.0 / heads) + LN_EPS)
+            total = jnp.sum(both, axis=0)
+            mean = total * (1.0 / row_count)
+            square = total + swap(per * jnp.sum((both - mean) ** 2, axis=0))
+            st_tot[u, 2, to] = jnp.where(lane < HALF, mean, lax.rsqrt(square * (1.0 / heads) + LN_EPS))
+        for q in range(1, row_count):
+            ref = st_tot.at[u, :, pl.ds(first, own)]
+            send(ref, ref, ag_s.at[u, q], ag_r.at[u, me], row=peers[q])
+
+    gain = g_ref[pl.ds(pl.multiple_of(me * per, 8), per), :]
+    low = lax.broadcasted_iota(jnp.int32, (per, LANES), 1) < HALF
+
+    def normalize(u):
+        for q in range(1, row_count):
+            ref = st_tot.at[u, :, pl.ds(pl.multiple_of(own * peers[q], 8), own)]
+            remote(ref, ref, ag_s.at[u, q], ag_r.at[u, peers[q]], row=peers[q]).wait_recv()
+        base = u * (per * pitch)
+
+        def wide(t, carry):
+            for s in range(8):
+                i = 8 * t + s
+                v = flat_wide[pl.ds(base + i, per, stride=pitch), :]
+                v = (v - st_tot[u, 0, pl.ds(i, 1)]) * st_tot[u, 1, pl.ds(i, 1)] * gain
+                y_out[t // 8, 2 * u + (t // 4) % 2, 8 * (t % 4) + s] = v.astype(BF16)
+            return carry
+
+        def tail(t, carry):
+            for s in range(8):
+                i = 32 * (t // 2) + 8 * (t % 2) + s
+                lo = flat_tail[pl.ds(base + i, per, stride=pitch), :]
+                hi = flat_tail[pl.ds(base + i + 16, per, stride=pitch), :]
+                first, second = st_tot[u, 2, pl.ds(i, 1)], st_tot[u, 2, pl.ds(i + 16, 1)]
+                v = jnp.where(low, lo, swap(hi))
+                mean = jnp.where(low[:1], first, swap(second))
+                rstd = jnp.where(low[:1], swap(first), second)
+                y_out[t // 4, 2 * u + (t // 2) % 2, 32 + 8 * (t % 2) + s] = ((v - mean) * rstd * gain).astype(BF16)
+            return carry
+
+        lax.fori_loop(0, rows // 8, wide, 0)
+        lax.fori_loop(0, rows // 16, tail, 0)
+
+    def back(u, begin):
+        for block in blocks:
+            for c, group, count, place, tag in MESSAGES[u]:
+                dest = block * 2 + c
+                src = y_out.at[block, pl.ds(group, count)]
+                dst = y_hbm.at[me, pl.ds(place, count)]
+
+                @pl.when(dest != me)
+                def _():
+                    copy = remote(src, dst, ys_s.at[block, c, tag], ys_r.at[me, tag], row=dest)
+                    copy.start() if begin else copy.wait_send()
+
+                @pl.when(dest == me)
+                def _():
+                    copy = pltpu.make_async_copy(src, dst, loc.at[4 + tag])
+                    copy.start() if begin else copy.wait()
+
+    scatter_a(0)
+    scatter_a(1)
+    scatter_b()
+    scatter_a(2)
+    direct(0)
+    forward(0, 0, row_count)
+    direct(1)
+    forward(1, 0, row_count)
+    spread()
+    arrived(0)
+    product(0)
+    partial(0)
+    direct(2)
+    combine(0)
+    arrived(1)
+    product(1)
+    partial(1)
+    normalize(0)
+    combine(1)
+    back(0, True)
+    forward(2, 0, row_count // 2)
+    normalize(1)
+    back(1, True)
+    forward(2, row_count // 2, row_count)
+    arrived(2)
+    product(2)
+    partial(2)
+    combine(2)
+    normalize(2)
+    back(2, True)
+
+    for copy in sends:
+        copy.wait_send()
+    for u in range(3):
+        back(u, False)
+    for c in range(2):
+        @pl.when(core == c)
+        def _():
+            for q in range(1, row_count):
+                for tag, (place, count) in enumerate(ARRIVALS[c]):
+                    ref = y_hbm.at[peers[q], pl.ds(place, count)]
+                    remote(y_out.at[0, pl.ds(0, count)], ref, ys_s.at[0, 0, tag], ys_r.at[peers[q], tag], row=peers[q]).wait_recv()
+
+
 def exchange(a, b, gain, row_count, col_count):
     heads, _, half, _ = a.shape
     per = heads // row_count
+    depth = row_count * half
+    rows = col_count * HALF
+    groups = 2 * half // 32
     wire = (row_count, per, 3, half, LANES)
-    got_a = lax.all_to_all(a.reshape(wire), 'row', 0, 0, tiled=True)
-    all_a = lax.all_gather(got_a, 'col', axis=0)
-    got_b = lax.all_to_all(b.reshape(wire), 'row', 0, 0, tiled=True)
-
-    def unpack(w):
-        w = jnp.moveaxis(w, -3, 0)
-        tail = jnp.stack([w[2, ..., :HALF], w[2, ..., HALF:]])
-        return jnp.concatenate([w[:2], tail], axis=-1)
-
-    left, right = unpack(all_a), unpack(got_b)
-    o = jnp.einsum('pyshki,pshkj->yhij', left, right, preferred_element_type=F32)
-    cols = o.shape[-1]
-    o = jnp.moveaxis(o, 1, 0).reshape(per, col_count * cols, cols)
-    mean_p = jnp.mean(o, axis=0)
-    m2_p = jnp.sum((o - mean_p) ** 2, axis=0)
-    mean = lax.pmean(mean_p, 'row')
-    m2 = lax.psum(m2_p + per * (mean_p - mean) ** 2, 'row')
-    g = lax.dynamic_slice_in_dim(gain, lax.axis_index('row') * per, per).astype(F32)
-    y = ((o - mean) * lax.rsqrt(m2 / heads + LN_EPS) * g[:, None, None]).astype(BF16)
-    y = jnp.transpose(y.reshape(per, row_count, 2 * half // 32, 32, cols), (1, 2, 3, 0, 4))
-    wide = y[..., :LANES]
-    narrow = jnp.concatenate([y[:, :, :16, :, LANES:], y[:, :, 16:, :, LANES:]], axis=-1)
-    packed = jnp.concatenate([wide, narrow], axis=2)
-    return lax.all_to_all(packed, 'row', 0, 0, tiled=True)
+    dma = pltpu.SemaphoreType.DMA
+    gains = jnp.broadcast_to(gain.astype(F32)[:, None], (heads, LANES))
+    hbm = pl.BlockSpec(memory_space=pl.ANY)
+    return pl.pallas_call(
+        functools.partial(exchange_kernel, row_count, col_count),
+        in_specs=[hbm, hbm, pl.BlockSpec(memory_space=pltpu.VMEM)],
+        out_specs=hbm,
+        out_shape=jax.ShapeDtypeStruct((row_count, groups, 48, per, LANES), BF16),
+        scratch_shapes=[
+            pltpu.VMEM((3, col_count, row_count, per, half, LANES), BF16),
+            pltpu.VMEM(wire, BF16),
+            pltpu.VMEM((per, 2, depth, 2 * LANES), BF16),
+            pltpu.VMEM((3, per, rows + 8, LANES), F32),
+            pltpu.VMEM((3, per, rows + 8, LANES), F32),
+            pltpu.VMEM((3, 3, rows, LANES), F32),
+            pltpu.VMEM((3, row_count, 3, rows // row_count, LANES), F32),
+            pltpu.VMEM((3, 3, rows, LANES), F32),
+            pltpu.VMEM((col_count, 2 * groups, 48, per, LANES), BF16),
+            dma((3, row_count)), dma((3, row_count)), dma((row_count,)), dma((row_count,)),
+            dma((3, 2, row_count)), dma((3, 2, row_count)), dma((3, row_count)), dma((3, row_count)),
+            dma((3, row_count)), dma((3, row_count)), dma((3, row_count)), dma((3, row_count)),
+            dma((col_count, 2, 2)), dma((row_count, 2)), dma((6,)),
+        ],
+        compiler_params=pltpu.CompilerParams(collective_id=0, has_side_effects=True, vmem_limit_bytes=62 * 2**20),
+        cost_estimate=pl.CostEstimate(flops=12 * per * depth * 2 * LANES * rows, bytes_accessed=a.size * 8, transcendentals=0),
+    )(a.reshape(wire), b.reshape(wire), gains)
 
 
 def solution(mesh):

time: 527 us -> 265 us (0.50)
  Pallas kernels: 52.4 us -> 255 us
  waiting for transfers between devices: 197 us -> 0 us
  blocking collectives: 176 us -> 0 us
  local copies, waits for them, and re-layouts: 49.3 us -> 6.82 us
  other arithmetic: 20.7 us -> 0.68 us
  matrix products: 13.8 us -> 0 us
  between operations: 13.3 us -> 0.05 us
    pallas_call x0 -> x1, Pallas kernels: none -> 207 us  [exchange(): pl.pallas_call(functools.partial(exchange_kernel, row_count, col_count),...]
    all_to_all x3 -> x0, blocking collectives: 176 us -> none  [the longest x1 59.4 us: exchange(): return lax.all_to_all(packed, 'row', 0, 0, tiled=True)]
    all_gather x1 -> x0, waiting for transfers between devices: 111 us -> none  [exchange(): all_a = lax.all_gather(got_a, 'col', axis=0)]
    psum x2 -> x0, waiting for transfers between devices: 86.4 us -> none  [the longest x1 46.8 us: exchange(): mean = lax.pmean(mean_p, 'row')]
    dot_general x1 -> x0, local copies, waits for them, and re-layouts: 16.3 us -> none  [exchange(): jnp.einsum('pyshki,pshkj->yhij', left, right, preferred_element_type=F32)]
    slice x7 -> x0, local copies, waits for them, and re-layouts: 15.3 us -> none  [the longest x2 8.81 us: unpack(): tail = jnp.stack([w[2, ..., :HALF], w[2, ..., HALF:]])]
    dot_general x1 -> x0, matrix products: 13.8 us -> none  [exchange(): jnp.einsum('pyshki,pshkj->yhij', left, right, preferred_element_type=F32)]
    all_gather x1 -> x0, local copies, waits for them, and re-layouts: 11.4 us -> none  [exchange(): all_a = lax.all_gather(got_a, 'col', axis=0)]
  transfers between devices with their start and end apart: 3 -> 0, of which waited for: 3 -> 0; matrix products, arithmetic and copies ran while one was open for 5% -> 0% of each run, Pallas kernels for 0% -> 0%
where the time goes in v3:
time: 265 us; the launch traced here: 263 us
  Pallas kernels  255 us (96%)
  local copies, waits for them, and re-layouts  6.82 us (3%)
    pallas_call x1, Pallas kernels, exchange(): pl.pallas_call(functools.partial(exchange_kernel, row_count, col_count),...  207 us
    pallas_call x1, Pallas kernels, project(): pl.pallas_call(project_kernel, grid=(steps,), in_specs=[tile_spec, pl.Blo...  30 us
    pallas_call x1, Pallas kernels, finish(): pl.pallas_call(finish_kernel, grid=(groups,), in_specs=[pl.BlockSpec((src...  18.4 us

profile of v3, /device:TPU:101, one launch (start us, length us, event | category | flops | bytes accessed | tf_op | source)
XLA Modules:
  0.0 262.6 jit_solution(12616303544678893129)
XLA Ops:
  0.0 0.9 copy.18
  0.9 0.9 copy.19
  1.7 0.9 copy.20
  2.6 0.9 copy.21
  3.5 0.7 maximum_bitcast_fusion.w_ref
  4.2 1.4 broadcast_in_dim.2.g_ref
  5.5 1.0 reshape.26
  6.5 0.1 copy.23
  6.7 0.2 reshape.33
  6.8 0.7 pad.4.clone
  7.5 30.0 %shard_map.100 = (bf16[2,48,192,128]{3,2,1,0:T(8,128)(2,1)}, bf16[128,3,48,128]{3,2,1,0:T(8,128)(2,1)}, bf16[128,3,48,128]{3,2,1,0:T(8,128)(2,1)}) custom-call(bf16[2,48,192,128]{3,2,1,0:T(8,128)(2,1)} %bitcast.9, s32[3,16,8,128]{3,2,1,0:T(8,128)} %bitcast.12, bf16[1,128]{1,0:T(2,128)(2,1)} %bitcast.13, bf16[512,128]{1,0:T(8,128)(2,1)} %maximum_bitcast_fusion.w_ref), custom_call_target="tpu_custom_call" | custom-call | flops 2415919104 | bytes 18874368 | tf_op jit(solution)/shard_map/pallas_call | solution.py:72
  37.6 206.6 %shard_map.101.y_ref = bf16[8,3,48,16,128]{4,3,2,1,0:T(8,128)(2,1)} custom-call(bf16[8,16,3,48,128]{4,3,2,1,0:T(8,128)(2,1)} %bitcast.14, bf16[8,16,3,48,128]{4,3,2,1,0:T(8,128)(2,1)} %bitcast.15, f32[128,128]{1,0:T(8,128)} %broadcast_in_dim.2.g_ref), custom_call_target="tpu_custom_call" | custom-call | flops 4831838208 | bytes 18874368 | tf_op jit(solution)/shard_map/pallas_call | solution.py:395
  244.2 18.4 %shard_map.102 = bf16[96,192,128]{2,1,0:T(8,128)(2,1)} custom-call(bf16[8,3,48,16,128]{4,3,2,1,0:T(8,128)(2,1)} %shard_map.101.y_ref, bf16[96,192,128]{2,1,0:T(8,128)(2,1)} %bitcast.10, bf16[96,192,128]{2,1,0:T(8,128)(2,1)} %z_ref.1, bf16[128,128]{1,0:T(8,128)(2,1)} %wg_ref.1, bf16[128,128]{1,0:T(8,128)(2,1)} %wo_ref.1), custom_call_target="tpu_custom_call" | custom-call | flops 1207959552 | bytes 18874368 | tf_op jit(solution)/shard_map/pallas_call | solution.py:120

commit v4 on v3

v4 whole, which is shorter than its diff:
```python
import functools

import jax
import jax.numpy as jnp
from jax import lax
from jax.experimental import pallas as pl
from jax.experimental.pallas import tpu as pltpu
from jax.sharding import PartitionSpec as P

LN_EPS = 0.00001
LANES = 128
HALF = 64
GROUP = 16
PITCH = 24
F32 = jnp.float32
BF16 = jnp.bfloat16


def dot(lhs, rhs, dims):
    return lax.dot_general(lhs, rhs, (dims, ((), ())), preferred_element_type=F32)


def layer_norm(values, gain):
    mean = jnp.mean(values, axis=-1, keepdims=True)
    centered = values - mean
    variance = jnp.mean(centered * centered, axis=-1, keepdims=True)
    return centered * lax.rsqrt(variance + LN_EPS) * gain


def finish_kernel(y_ref, x_ref, z_ref, wg_ref, wo_ref, out_ref):
    srcs, _, _, per, _ = y_ref.shape
    heads = srcs * per

    def update(pos):
        return dot(y_ref[:, 0, pos].reshape(heads, LANES), wo_ref[...], ((0,), (0,)))

    def gated(x, z, upd):
        gate = jax.nn.sigmoid(dot(x, wg_ref[...], ((1,), (0,))))
        return (z.astype(F32) + gate * upd).astype(BF16)

    def wide(t, carry):
        out_ref[t, :LANES] = gated(x_ref[t, :LANES], z_ref[t, :LANES], update(t))
        return carry

    def narrow(t, carry):
        x = jnp.concatenate([x_ref[t, LANES:], x_ref[t + 16, LANES:]], axis=0)
        z = jnp.concatenate([z_ref[t, LANES:], z_ref[t + 16, LANES:]], axis=0)
        res = gated(x, z, update(t + 32))
        out_ref[t, LANES:] = res[:HALF]
        out_ref[t + 16, LANES:] = res[HALF:]
        return carry

    lax.fori_loop(0, 32, wide, 0, unroll=2)
    lax.fori_loop(0, 16, narrow, 0, unroll=2)


def finish(y, x, z, w_gate, w_out):
    rows, cols, chan = z.shape
    srcs, groups, places, per, _ = y.shape
    tile_spec = pl.BlockSpec((32, cols, chan), lambda t: (t, 0, 0))
    return pl.pallas_call(
        finish_kernel,
        grid=(groups,),
        in_specs=[
            pl.BlockSpec((srcs, 1, places, per, LANES), lambda t: (0, t, 0, 0, 0)),
            tile_spec,
            tile_spec,
            pl.BlockSpec(w_gate.shape, lambda t: (0, 0)),
            pl.BlockSpec(w_out.shape, lambda t: (0, 0)),
        ],
        out_specs=tile_spec,
        out_shape=jax.ShapeDtypeStruct(z.shape, BF16),
        compiler_params=pltpu.CompilerParams(vmem_limit_bytes=60 * 2**20),
        cost_estimate=pl.CostEstimate(flops=4 * rows * cols * chan * chan, bytes_accessed=rows * cols * chan * 8, transcendentals=0),
    )(y, x.reshape(z.shape), z, w_gate, w_out)


def remote(src, dst, send_sem, recv_sem, **place):
    return pltpu.make_async_remote_copy(
        src_ref=src, dst_ref=dst, send_sem=send_sem, recv_sem=recv_sem, device_id=place, device_id_type=pl.DeviceIdType.MESH
    )


MESSAGES = (((0, 0, 2, 0, 0),), ((0, 2, 1, 2, 1), (1, 3, 1, 0, 0)), ((1, 4, 2, 1, 1),))
ARRIVALS = (((0, 2), (2, 1)), ((0, 1), (1, 2)))


def exchange_kernel(
    row_count, col_count, z_hbm, m_ref, gi_ref, wa_ref, wag_ref, wb_ref, wbg_ref, go_ref, y_hbm, x_hbm,
    zx, weights, keep, gains, turn, a_out, b_out, all_a, got_b, rhs, o_wide, o_tail, st_part, st_got, st_tot, y_out,
    xa_s, xa_r, xb_s, xb_r, dir_s, dir_r, fwd_s, fwd_r, rs_s, rs_r, ag_s, ag_r, ys_s, ys_r, loc,
):
    me, col = lax.axis_index('row'), lax.axis_index('col')
    per, _, half, _ = a_out.shape[1:]
    heads = per * row_count
    depth = row_count * half
    chip, core = me // 2, me % 2
    chips = row_count // 2
    steps = [(0, 0), (0, 1)]
    for d in range(1, chips // 2 + 1):
        steps += [(d, 0), (-d, 0), (d, 1), (-d, 1)] if 2 * d < chips else [(d, 0), (d, 1)]
    peers = [lax.rem(chip + d + chips, chips) * 2 + lax.rem(core + f, 2) for d, f in steps]
    up, down = lax.rem(col + 1, col_count), lax.rem(col + col_count - 1, col_count)
    far = lax.rem(col + 2, col_count)
    order = (col, down, up, far)

    loads = [pltpu.make_async_copy(z_hbm.at[:, :, pl.ds(HALF * s, HALF)], zx.at[s], loc.at[s]) for s in range(3)]
    saves = [pltpu.make_async_copy(zx.at[s], x_hbm.at[:, :, pl.ds(HALF * s, HALF)], loc.at[3 + s]) for s in range(3)]
    for copy in loads:
        copy.start()
    barrier = pltpu.get_barrier_semaphore()
    for p in peers[1:]:
        pl.semaphore_signal(barrier, inc=1, device_id={'row': p}, device_id_type=pl.DeviceIdType.MESH)
    for p in (up, down):
        pl.semaphore_signal(barrier, inc=1, device_id={'col': p}, device_id_type=pl.DeviceIdType.MESH)

    for n, ref in enumerate((wa_ref, wag_ref, wb_ref, wbg_ref)):
        weights[n * heads:(n + 1) * heads] = ref[...].T
    gains[...] = jnp.broadcast_to(go_ref[...].astype(F32), (heads, heads)).T
    gain_in = gi_ref[...].astype(F32)
    mask = m_ref[...].astype(F32)
    low_mask, high_mask = mask[:half], mask[half:]
    for s in range(3):
        at = slice(HALF * s, HALF * (s + 1))
        keep[s] = jnp.concatenate([low_mask[:, at], high_mask[:, at]], axis=1)

    flat_turn = turn.reshape(2 * heads * PITCH, LANES)
    flat_out = [ref.reshape(heads, 3, half, LANES) for ref in (a_out, b_out)]

    def project(s, sides, fresh):
        def group(g, carry):
            def row(t, carry):
                k = g * GROUP + t
                tall = jnp.concatenate([zx[s, 0, k], zx[s, 1, k]], axis=0)
                if fresh:
                    tall = layer_norm(tall.astype(F32), gain_in).astype(BF16)
                    zx[s, 0, k] = tall[:HALF]
                    zx[s, 1, k] = tall[HALF:]
                for side in sides:
                    both = dot(weights[2 * side * heads:2 * (side + 1) * heads], tall, ((1,), (1,)))
                    act = keep[s, pl.ds(k, 1)] * jax.nn.sigmoid(both[heads:]) * both[:heads]
                    flat_turn[pl.ds(side * heads * PITCH + t, heads, stride=PITCH), :] = act
                return carry

            lax.fori_loop(0, GROUP, row, 0, unroll=2)

            def pack(h, carry):
                for side in sides:
                    flat_out[side][h, s, pl.ds(pl.multiple_of(g * GROUP, GROUP), GROUP)] = turn[side * heads + h, 0:GROUP].astype(BF16)
                return carry

            lax.fori_loop(0, heads, pack, 0, unroll=4)
            return carry

        lax.fori_loop(0, half // GROUP, group, 0)

    sends = []

    def send(*args, **place):
        copy = remote(*args, **place)
        copy.start()
        sends.append(copy)

    def scatter_a(s):
        for q in range(1, row_count):
            send(a_out.at[peers[q], :, s], all_a.at[s, col, me], xa_s.at[s, q], xa_r.at[s, me], row=peers[q])
        all_a[s, col, me] = a_out[me, :, s]

    def scatter_b():
        for q in range(1, row_count):
            send(b_out.at[peers[q]], got_b.at[me], xb_s.at[q], xb_r.at[me], row=peers[q])
        got_b[me] = b_out[me]

    def direct(s, first, last):
        for q in range(first, last):
            src = all_a.at[s, col, peers[q]]
            if q:
                remote(src, src, xa_s.at[s, q], xa_r.at[s, peers[q]], row=peers[q]).wait_recv()
            send(src, src, dir_s.at[s, 0, q], dir_r.at[s, 0, peers[q]], col=up)
            send(src, src, dir_s.at[s, 1, q], dir_r.at[s, 1, peers[q]], col=down)

    def forward(s, first, last):
        for q in range(first, last):
            for way, block in ((0, down), (1, up)):
                ref = all_a.at[s, block, peers[q]]
                remote(ref, ref, dir_s.at[s, way, q], dir_r.at[s, way, peers[q]], col=up).wait_recv()
            away, block = (up, down) if q % 2 == 0 else (down, up)
            src = all_a.at[s, block, peers[q]]
            send(src, src, fwd_s.at[s, q], fwd_r.at[s, peers[q]], col=away)

    def arrived(s):
        for q in range(row_count):
            ref = all_a.at[s, far, peers[q]]
            remote(ref, ref, fwd_s.at[s, q], fwd_r.at[s, peers[q]], col=up).wait_recv()

    lane = lax.broadcasted_iota(jnp.int32, (8, LANES), 1)
    pitch = o_wide.shape[2]
    flat_wide = o_wide.reshape(2 * per * pitch, LANES)
    flat_tail = o_tail.reshape(2 * per * pitch, LANES)

    def swap(v):
        return pltpu.roll(v, HALF, v.ndim - 1)

    def spread():
        for q in range(1, row_count):
            ref = got_b.at[peers[q]]
            remote(ref, ref, xb_s.at[q], xb_r.at[peers[q]], row=peers[q]).wait_recv()

        def channel(h, carry):
            w = [got_b[:, h, s].reshape(depth, LANES) for s in range(3)]
            rhs[h, 0, :, :LANES] = jnp.concatenate([w[0][:, :HALF], w[1][:, :HALF]], axis=1)
            rhs[h, 1, :, :LANES] = jnp.concatenate([w[0][:, HALF:], w[1][:, HALF:]], axis=1)
            rhs[h, 0, :, LANES:] = w[2]
            rhs[h, 1, :, LANES:] = jnp.concatenate([w[2][:, HALF:], w[2][:, :HALF]], axis=1)
            return carry

        lax.fori_loop(0, per, channel, 0)

    def product(u, s, first, count):
        at = slice(first * HALF, (first + count) * HALF)

        def channel(h, carry):
            turned = [all_a[s, c, :, h].reshape(depth, LANES).T for c in order[first:first + count]]
            res = dot(jnp.concatenate([t[:HALF] for t in turned], axis=0), rhs[h, 0], ((1,), (0,)))
            res += dot(jnp.concatenate([t[HALF:] for t in turned], axis=0), rhs[h, 1], ((1,), (0,)))
            o_wide[s % 2, h, at] = res[:, :LANES]
            o_tail[s % 2, h, at] = res[:, LANES:]
            return carry

        lax.fori_loop(0, per, channel, 0)

    def partial(u, s, first, count):
        def tile(t, carry):
            at = pl.ds(pl.multiple_of(first * HALF + 8 * t, 8), 8)
            out = []
            for ref in (o_wide, o_tail):
                v = ref[s % 2, :, at]
                mean = jnp.sum(v, axis=0) * (1.0 / per)
                out += [mean, jnp.sum((v - mean) ** 2, axis=0)]
            st_part[s, 0, at] = out[0]
            st_part[s, 1, at] = out[1]
            st_part[s, 2, at] = jnp.where(lane < HALF, out[2], swap(out[3]))
            return carry

        lax.fori_loop(0, count * HALF // 8, tile, 0, unroll=2)
        own = count * HALF // row_count
        for q in range(1, row_count):
            at = pl.ds(pl.multiple_of(first * HALF + own * peers[q], 8), own)
            send(st_part.at[s, :, at], st_got.at[u, me, :, 0:own], rs_s.at[u, q], rs_r.at[u, me], row=peers[q])

    def combine(u, s, first, count):
        own = count * HALF // row_count
        base = pl.multiple_of(first * HALF + own * me, 8)
        st_got[u, me, :, 0:own] = st_part[s, :, pl.ds(base, own)]
        for q in range(1, row_count):
            ref = st_got.at[u, peers[q], :, 0:own]
            remote(ref, ref, rs_s.at[u, q], rs_r.at[u, peers[q]], row=peers[q]).wait_recv()
        for t in range(own // 8):
            at = slice(8 * t, 8 * t + 8)
            to = pl.ds(pl.multiple_of(base + 8 * t, 8), 8)
            means, squares, both = st_got[u, :, 0, at], st_got[u, :, 1, at], st_got[u, :, 2, at]
            mean = jnp.sum(means, axis=0) * (1.0 / row_count)
            square = jnp.sum(squares, axis=0) + per * jnp.sum((means - mean) ** 2, axis=0)
            st_tot[s, 0, to] = mean
            st_tot[s, 1, to] = lax.rsqrt(square * (1.0 / heads) + LN_EPS)
            total = jnp.sum(both, axis=0)
            mean = total * (1.0 / row_count)
            square = total + swap(per * jnp.sum((both - mean) ** 2, axis=0))
            st_tot[s, 2, to] = jnp.where(lane < HALF, mean, lax.rsqrt(square * (1.0 / heads) + LN_EPS))
        for q in range(1, row_count):
            ref = st_tot.at[s, :, pl.ds(base, own)]
            send(ref, ref, ag_s.at[u, q], ag_r.at[u, me], row=peers[q])

    gain_out = gains[pl.ds(pl.multiple_of(me * per, 8), per), :]
    low = lax.broadcasted_iota(jnp.int32, (per, LANES), 1) < HALF

    def normalize(u, s, first, count):
        own = count * HALF // row_count
        for q in range(1, row_count):
            ref = st_tot.at[s, :, pl.ds(pl.multiple_of(first * HALF + own * peers[q], 8), own)]
            remote(ref, ref, ag_s.at[u, q], ag_r.at[u, peers[q]], row=peers[q]).wait_recv()
        base = (s % 2) * (per * pitch)

        def wide(t, carry):
            for r in range(8):
                i = 8 * t + r
                v = flat_wide[pl.ds(base + i, per, stride=pitch), :]
                v = (v - st_tot[s, 0, pl.ds(i, 1)]) * st_tot[s, 1, pl.ds(i, 1)] * gain_out
                y_out[t // 8, 2 * s + (t // 4) % 2, 8 * (t % 4) + r] = v.astype(BF16)
            return carry

        def tail(t, carry):
            for r in range(8):
                i = 32 * (t // 2) + 8 * (t % 2) + r
                lo = flat_tail[pl.ds(base + i, per, stride=pitch), :]
                hi = flat_tail[pl.ds(base + i + 16, per, stride=pitch), :]
                one, two = st_tot[s, 2, pl.ds(i, 1)], st_tot[s, 2, pl.ds(i + 16, 1)]
                v = jnp.where(low, lo, swap(hi))
                mean = jnp.where(low[:1], one, swap(two))
                rstd = jnp.where(low[:1], swap(one), two)
                y_out[t // 4, 2 * s + (t // 2) % 2, 32 + 8 * (t % 2) + r] = ((v - mean) * rstd * gain_out).astype(BF16)
            return carry

        lax.fori_loop(8 * first, 8 * (first + count), wide, 0)
        lax.fori_loop(4 * first, 4 * (first + count), tail, 0)

    def back(u, s, first, count, begin=True):
        for n in range(first, first + count):
            for c, group, size, place, tag in MESSAGES[s]:
                dest = order[n] * 2 + c
                src = y_out.at[n, pl.ds(group, size)]
                dst = y_hbm.at[me, pl.ds(place, size)]

                @pl.when(dest != me)
                def _():
                    copy = remote(src, dst, ys_s.at[n, c, tag], ys_r.at[me, tag], row=dest)
                    copy.start() if begin else copy.wait_send()

                @pl.when(dest == me)
                def _():
                    copy = pltpu.make_async_copy(src, dst, loc.at[6 + tag])
                    copy.start() if begin else copy.wait()

    units = [(0, 0, 0, col_count), (1, 1, 0, col_count), (2, 2, 0, col_count - 1), (3, 2, col_count - 1, 1)]

    loads[0].wait()
    project(0, (0,), True)
    pl.semaphore_wait(barrier, row_count + 1)
    scatter_a(0)
    direct(0, 0, 1)
    loads[1].wait()
    project(1, (0,), True)
    scatter_a(1)
    direct(0, 1, 4)
    project(0, (1,), False)
    project(1, (1,), False)
    direct(0, 4, 6)
    loads[2].wait()
    project(2, (0, 1), True)
    scatter_b()
    scatter_a(2)
    for copy in saves:
        copy.start()
    direct(0, 6, row_count)
    forward(0, 0, row_count)
    direct(1, 0, row_count)
    forward(1, 0, row_count)
    spread()
    arrived(0)
    product(*units[0])
    partial(*units[0])
    direct(2, 0, row_count)
    combine(*units[0])
    arrived(1)
    product(*units[1])
    partial(*units[1])
    normalize(*units[0])
    combine(*units[1])
    back(*units[0])
    forward(2, 0, row_count // 2)
    normalize(*units[1])
    back(*units[1])
    forward(2, row_count // 2, row_count)
    product(*units[2])
    partial(*units[2])
    combine(*units[2])
    arrived(2)
    product(*units[3])
    partial(*units[3])
    normalize(*units[2])
    combine(*units[3])
    back(*units[2])
    normalize(*units[3])
    back(*units[3])

    for copy in saves:
        copy.wait()
    for copy in sends:
        copy.wait_send()
    for unit in units:
        back(*unit, begin=False)
    for c in range(2):
        @pl.when(core == c)
        def _():
            for q in range(1, row_count):
                for tag, (place, size) in enumerate(ARRIVALS[c]):
                    ref = y_hbm.at[peers[q], pl.ds(place, size)]
                    remote(y_out.at[0, pl.ds(0, size)], ref, ys_s.at[0, 0, tag], ys_r.at[peers[q], tag], row=peers[q]).wait_recv()


def exchange(z, mask, g_in, w_a, w_ag, w_b, w_bg, g_out, row_count, col_count):
    tile_rows, cols, chan = z.shape
    heads = w_a.shape[1]
    half = tile_rows // 2
    per = heads // row_count
    depth = row_count * half
    rows = col_count * HALF
    groups = tile_rows // 32
    wire = (row_count, per, 3, half, LANES)
    dma = pltpu.SemaphoreType.DMA
    hbm = pl.BlockSpec(memory_space=pl.ANY)
    vmem = pl.BlockSpec(memory_space=pltpu.VMEM)
    return pl.pallas_call(
        functools.partial(exchange_kernel, row_count, col_count),
        in_specs=[hbm] + [vmem] * 7,
        out_specs=[hbm, hbm],
        out_shape=[
            jax.ShapeDtypeStruct((row_count, groups, 48, per, LANES), BF16),
            jax.ShapeDtypeStruct((2, half, cols, chan), BF16),
        ],
        scratch_shapes=[
            pltpu.VMEM((3, 2, half, HALF, chan), BF16),
            pltpu.VMEM((4 * heads, chan), BF16),
            pltpu.VMEM((3, half, LANES), F32),
            pltpu.VMEM((heads, LANES), F32),
            pltpu.VMEM((2 * heads, PITCH, LANES), F32),
            pltpu.VMEM(wire, BF16),
            pltpu.VMEM(wire, BF16),
            pltpu.VMEM((3, col_count, row_count, per, half, LANES), BF16),
            pltpu.VMEM(wire, BF16),
            pltpu.VMEM((per, 2, depth, 2 * LANES), BF16),
            pltpu.VMEM((2, per, rows + 8, LANES), F32),
            pltpu.VMEM((2, per, rows + 8, LANES), F32),
            pltpu.VMEM((3, 3, rows, LANES), F32),
            pltpu.VMEM((4, row_count, 3, rows // row_count, LANES), F32),
            pltpu.VMEM((3, 3, rows, LANES), F32),
            pltpu.VMEM((col_count, 2 * groups, 48, per, LANES), BF16),
            dma((3, row_count)), dma((3, row_count)), dma((row_count,)), dma((row_count,)),
            dma((3, 2, row_count)), dma((3, 2, row_count)), dma((3, row_count)), dma((3, row_count)),
            dma((4, row_count)), dma((4, row_count)), dma((4, row_count)), dma((4, row_count)),
            dma((col_count, 2, 2)), dma((row_count, 2)), dma((8,)),
        ],
        compiler_params=pltpu.CompilerParams(collective_id=0, has_side_effects=True, vmem_limit_bytes=67000000),
        cost_estimate=pl.CostEstimate(flops=12 * per * depth * 2 * LANES * rows, bytes_accessed=z.size * 8, transcendentals=0),
    )(z.reshape(2, half, cols, chan), mask, g_in.reshape(1, chan), w_a, w_ag, w_b, w_bg, g_out.reshape(1, heads))


def solution(mesh):
    row_count = mesh.shape['row']
    col_count = mesh.shape['col']
    tile_spec = P(('batch', 'row'), 'col', None)
    mask_spec = P(('batch', 'row'), 'col')

    def local_step(z, mask, g_in, w_a, w_ag, w_b, w_bg, w_g, g_out, w_o):
        y, x = exchange(z, mask, g_in, w_a, w_ag, w_b, w_bg, g_out, row_count, col_count)
        return finish(y, x, z, w_g, w_o)

    return jax.shard_map(local_step, mesh=mesh, in_specs=(tile_spec, mask_spec) + (P(),) * 8, out_specs=tile_spec, check_vma=False)
```

time: 265 us -> 238 us (0.90)
  Pallas kernels: 255 us -> 238 us
  local copies, waits for them, and re-layouts: 6.82 us -> 0 us
    pallas_call x1 -> x0, Pallas kernels: 30 us -> none  [project(): pl.pallas_call(project_kernel, grid=(steps,), in_specs=[tile_spec, pl.Blo...]
    pallas_call x1, Pallas kernels: 207 us -> 220 us  [exchange(): pl.pallas_call(functools.partial(exchange_kernel, row_count, col_count),...]
    unnamed x6 -> x0, local copies, waits for them, and re-layouts: 3.75 us -> none
where the time goes in v4:
time: 238 us
  Pallas kernels  238 us (100%)
    pallas_call x1, Pallas kernels, exchange(): pl.pallas_call(functools.partial(exchange_kernel, row_count, col_count),...  220 us
    pallas_call x1, Pallas kernels, finish(): pl.pallas_call(finish_kernel, grid=(groups,), in_specs=[pl.BlockSpec((src...  18.4 us

profile of v4, /device:TPU:101, one launch (start us, length us, event | category | flops | bytes accessed | tf_op | source)
XLA Modules:
  0.0 237.9 jit_solution(795390384138690611)
XLA Ops:
  0.0 219.5 %shard_map.100 = (bf16[8,3,48,16,128]{4,3,2,1,0:T(8,128)(2,1)}, bf16[2,48,192,128]{3,2,1,0:T(8,128)(2,1)}) custom-call(bf16[2,48,192,128]{3,2,1,0:T(8,128)(2,1)} %bitcast.4, s32[96,192]{1,0:T(8,128)} %m_ref.1, bf16[1,128]{1,0:T(2,128)(2,1)} %bitcast.6, bf16[128,128]{1,0:T(8,128)(2,1)} %wa_ref.1, bf16[128,128]{1,0:T(8,128)(2,1)} %wag_ref.1, ...), custom_call_target="tpu_custom_call" | custom-call | flops 4831838208 | bytes 18874368 | tf_op jit(solution)/shard_map/pallas_call | solution.py:403
  219.5 18.4 %shard_map.101 = bf16[96,192,128]{2,1,0:T(8,128)(2,1)} custom-call(bf16[8,3,48,16,128]{4,3,2,1,0:T(8,128)(2,1)} %get-tuple-element.7.y_ref, bf16[96,192,128]{2,1,0:T(8,128)(2,1)} %bitcast.5, bf16[96,192,128]{2,1,0:T(8,128)(2,1)} %z_ref.1, bf16[128,128]{1,0:T(8,128)(2,1)} %wg_ref.1, bf16[128,128]{1,0:T(8,128)(2,1)} %wo_ref.1), custom_call_target="tpu_custom_call" | custom-call | flops 1207959552 | bytes 18874368 | tf_op jit(solution)/shard_map/pallas_call | solution.py:61

commit v5 on v4

--- a/solution.py
+++ b/solution.py
@@ -12,6 +12,10 @@
 HALF = 64
 GROUP = 16
 PITCH = 24
+BATCH = 16
+QUART = 32
+PAIR = 2
+UNROLL = 4
 F32 = jnp.float32
 BF16 = jnp.bfloat16
 
@@ -31,27 +35,33 @@
     srcs, _, _, per, _ = y_ref.shape
     heads = srcs * per
 
-    def update(pos):
-        return dot(y_ref[:, 0, pos].reshape(heads, LANES), wo_ref[...], ((0,), (0,)))
-
     def gated(x, z, upd):
         gate = jax.nn.sigmoid(dot(x, wg_ref[...], ((1,), (0,))))
         return (z.astype(F32) + gate * upd).astype(BF16)
 
-    def wide(t, carry):
-        out_ref[t, :LANES] = gated(x_ref[t, :LANES], z_ref[t, :LANES], update(t))
+    def wide(i, carry):
+        t = BATCH * i
+        at = pl.ds(t, BATCH)
+        turned = jnp.concatenate([y_ref[:, 0, t + r].reshape(heads, LANES) for r in range(BATCH)], axis=1)
+        upd = dot(turned, wo_ref[...], ((0,), (0,)))
+        x = jnp.concatenate([x_ref[s, at] for s in range(2)], axis=1).reshape(BATCH * LANES, LANES)
+        parts = [slice(QUART * n, QUART * (n + 1)) for n in (0, 3, 1, 4)]
+        z = jnp.concatenate([z_ref[at, part] for part in parts], axis=1).reshape(BATCH * LANES, LANES)
+        res = gated(x, z, upd).reshape(BATCH, LANES, LANES)
+        for e, part in enumerate(parts):
+            out_ref[at, part] = res[:, QUART * e:QUART * (e + 1)]
         return carry
 
-    def narrow(t, carry):
-        x = jnp.concatenate([x_ref[t, LANES:], x_ref[t + 16, LANES:]], axis=0)
-        z = jnp.concatenate([z_ref[t, LANES:], z_ref[t + 16, LANES:]], axis=0)
-        res = gated(x, z, update(t + 32))
-        out_ref[t, LANES:] = res[:HALF]
-        out_ref[t + 16, LANES:] = res[HALF:]
-        return carry
-
-    lax.fori_loop(0, 32, wide, 0, unroll=2)
-    lax.fori_loop(0, 16, narrow, 0, unroll=2)
+    lax.fori_loop(0, 32 // BATCH, wide, 0)
+    turned = jnp.concatenate([y_ref[:, 0, 32 + r].reshape(heads, LANES) for r in range(16)], axis=1)
+    upd = dot(turned, wo_ref[...], ((0,), (0,)))
+    rows = [r + 16 * h for r in range(16) for h in range(2)]
+    x = jnp.concatenate([x_ref[2, p] for p in rows], axis=0)
+    z = jnp.concatenate([z_ref[p, QUART * n:QUART * (n + 1)] for p in rows for n in (2, 5)], axis=0)
+    res = gated(x, z, upd)
+    for e, p in enumerate(rows):
+        for n in range(2):
+            out_ref[p, QUART * (2 + 3 * n):QUART * (3 + 3 * n)] = res[HALF * e + QUART * n:HALF * e + QUART * (n + 1)]
 
 
 def finish(y, x, z, w_gate, w_out):
@@ -63,7 +73,7 @@
         grid=(groups,),
         in_specs=[
             pl.BlockSpec((srcs, 1, places, per, LANES), lambda t: (0, t, 0, 0, 0)),
-            tile_spec,
+            pl.BlockSpec((3, 32, HALF, chan), lambda t: (0, t, 0, 0)),
             tile_spec,
             pl.BlockSpec(w_gate.shape, lambda t: (0, 0)),
             pl.BlockSpec(w_out.shape, lambda t: (0, 0)),
@@ -72,17 +82,13 @@
         out_shape=jax.ShapeDtypeStruct(z.shape, BF16),
         compiler_params=pltpu.CompilerParams(vmem_limit_bytes=60 * 2**20),
         cost_estimate=pl.CostEstimate(flops=4 * rows * cols * chan * chan, bytes_accessed=rows * cols * chan * 8, transcendentals=0),
-    )(y, x.reshape(z.shape), z, w_gate, w_out)
+    )(y, x.reshape(3, rows, HALF, chan), z, w_gate, w_out)
 
 
 def remote(src, dst, send_sem, recv_sem, **place):
     return pltpu.make_async_remote_copy(
         src_ref=src, dst_ref=dst, send_sem=send_sem, recv_sem=recv_sem, device_id=place, device_id_type=pl.DeviceIdType.MESH
     )
-
-
-MESSAGES = (((0, 0, 2, 0, 0),), ((0, 2, 1, 2, 1), (1, 3, 1, 0, 0)), ((1, 4, 2, 1, 1),))
-ARRIVALS = (((0, 2), (2, 1)), ((0, 1), (1, 2)))
 
 
 def exchange_kernel(
@@ -104,10 +110,22 @@
     far = lax.rem(col + 2, col_count)
     order = (col, down, up, far)
 
-    loads = [pltpu.make_async_copy(z_hbm.at[:, :, pl.ds(HALF * s, HALF)], zx.at[s], loc.at[s]) for s in range(3)]
-    saves = [pltpu.make_async_copy(zx.at[s], x_hbm.at[:, :, pl.ds(HALF * s, HALF)], loc.at[3 + s]) for s in range(3)]
-    for copy in loads:
-        copy.start()
+    loads = [
+        [
+            pltpu.make_async_copy(z_hbm.at[:, :, pl.ds(QUART * (s + 3 * e), QUART)], zx.at[s, :, :, pl.ds(QUART * e, QUART)], loc.at[s, e])
+            for e in range(2)
+        ]
+        for s in range(3)
+    ]
+    saves = [pltpu.make_async_copy(zx.at[s], x_hbm.at[s], loc.at[s, 2]) for s in range(3)]
+    for pair in loads:
+        for copy in pair:
+            copy.start()
+
+    def loaded(s):
+        for copy in loads[s]:
+            copy.wait()
+
     barrier = pltpu.get_barrier_semaphore()
     for p in peers[1:]:
         pl.semaphore_signal(barrier, inc=1, device_id={'row': p}, device_id_type=pl.DeviceIdType.MESH)
@@ -121,38 +139,44 @@
     mask = m_ref[...].astype(F32)
     low_mask, high_mask = mask[:half], mask[half:]
     for s in range(3):
-        at = slice(HALF * s, HALF * (s + 1))
-        keep[s] = jnp.concatenate([low_mask[:, at], high_mask[:, at]], axis=1)
+        keep[s] = jnp.concatenate([m[:, QUART * n:QUART * (n + 1)] for m in (low_mask, high_mask) for n in (s, s + 3)], axis=1)
 
     flat_turn = turn.reshape(2 * heads * PITCH, LANES)
     flat_out = [ref.reshape(heads, 3, half, LANES) for ref in (a_out, b_out)]
 
-    def project(s, sides, fresh):
-        def group(g, carry):
-            def row(t, carry):
+    def project(s, sides, fresh, between=()):
+        if fresh:
+            def norm(i, carry):
+                at = pl.ds(4 * i, 4)
+                v = zx[s, :, at].astype(F32).reshape(4 * LANES, heads)
+                zx[s, :, at] = layer_norm(v, gain_in).astype(BF16).reshape(2, 4, HALF, heads)
+                return carry
+
+            lax.fori_loop(0, half // 4, norm, 0)
+
+        for g in range(half // GROUP):
+            def row(i, carry):
+                t = PAIR * i
                 k = g * GROUP + t
-                tall = jnp.concatenate([zx[s, 0, k], zx[s, 1, k]], axis=0)
-                if fresh:
-                    tall = layer_norm(tall.astype(F32), gain_in).astype(BF16)
-                    zx[s, 0, k] = tall[:HALF]
-                    zx[s, 1, k] = tall[HALF:]
+                tall = jnp.concatenate([zx[s, e, k + r] for r in range(PAIR) for e in range(2)], axis=0)
                 for side in sides:
                     both = dot(weights[2 * side * heads:2 * (side + 1) * heads], tall, ((1,), (1,)))
-                    act = keep[s, pl.ds(k, 1)] * jax.nn.sigmoid(both[heads:]) * both[:heads]
-                    flat_turn[pl.ds(side * heads * PITCH + t, heads, stride=PITCH), :] = act
+                    for r in range(PAIR):
+                        at = slice(LANES * r, LANES * (r + 1))
+                        act = keep[s, pl.ds(k + r, 1)] * jax.nn.sigmoid(both[heads:, at]) * both[:heads, at]
+                        flat_turn[pl.ds(side * heads * PITCH + t + r, heads, stride=PITCH), :] = act
                 return carry
 
-            lax.fori_loop(0, GROUP, row, 0, unroll=2)
+            lax.fori_loop(0, GROUP // PAIR, row, 0, unroll=2)
 
             def pack(h, carry):
                 for side in sides:
-                    flat_out[side][h, s, pl.ds(pl.multiple_of(g * GROUP, GROUP), GROUP)] = turn[side * heads + h, 0:GROUP].astype(BF16)
+                    flat_out[side][h, s, g * GROUP:(g + 1) * GROUP] = turn[side * heads + h, 0:GROUP].astype(BF16)
                 return carry
 
-            lax.fori_loop(0, heads, pack, 0, unroll=4)
-            return carry
-
-        lax.fori_loop(0, half // GROUP, group, 0)
+            lax.fori_loop(0, heads, pack, 0, unroll=8)
+            if g < len(between):
+                between[g]()
 
     sends = []
 
@@ -214,7 +238,7 @@
             rhs[h, 1, :, LANES:] = jnp.concatenate([w[2][:, HALF:], w[2][:, :HALF]], axis=1)
             return carry
 
-        lax.fori_loop(0, per, channel, 0)
+        lax.fori_loop(0, per, channel, 0, unroll=UNROLL)
 
     def product(u, s, first, count):
         at = slice(first * HALF, (first + count) * HALF)
@@ -227,7 +251,7 @@
             o_tail[s % 2, h, at] = res[:, LANES:]
             return carry
 
-        lax.fori_loop(0, per, channel, 0)
+        lax.fori_loop(0, per, channel, 0, unroll=UNROLL)
 
     def partial(u, s, first, count):
         def tile(t, carry):
@@ -242,7 +266,7 @@
             st_part[s, 2, at] = jnp.where(lane < HALF, out[2], swap(out[3]))
             return carry
 
-        lax.fori_loop(0, count * HALF // 8, tile, 0, unroll=2)
+        lax.fori_loop(0, count * HALF // 8, tile, 0, unroll=UNROLL)
         own = count * HALF // row_count
         for q in range(1, row_count):
             at = pl.ds(pl.multiple_of(first * HALF + own * peers[q], 8), own)
@@ -286,7 +310,7 @@
                 i = 8 * t + r
                 v = flat_wide[pl.ds(base + i, per, stride=pitch), :]
                 v = (v - st_tot[s, 0, pl.ds(i, 1)]) * st_tot[s, 1, pl.ds(i, 1)] * gain_out
-                y_out[t // 8, 2 * s + (t // 4) % 2, 8 * (t % 4) + r] = v.astype(BF16)
+                y_out[t // 8, s + 3 * ((t // 4) % 2), 8 * (t % 4) + r] = v.astype(BF16)
             return carry
 
         def tail(t, carry):
@@ -298,50 +322,50 @@
                 v = jnp.where(low, lo, swap(hi))
                 mean = jnp.where(low[:1], one, swap(two))
                 rstd = jnp.where(low[:1], swap(one), two)
-                y_out[t // 4, 2 * s + (t // 2) % 2, 32 + 8 * (t % 2) + r] = ((v - mean) * rstd * gain_out).astype(BF16)
+                y_out[t // 4, s + 3 * ((t // 2) % 2), 32 + 8 * (t % 2) + r] = ((v - mean) * rstd * gain_out).astype(BF16)
             return carry
 
-        lax.fori_loop(8 * first, 8 * (first + count), wide, 0)
-        lax.fori_loop(4 * first, 4 * (first + count), tail, 0)
+        lax.fori_loop(8 * first, 8 * (first + count), wide, 0, unroll=UNROLL)
+        lax.fori_loop(4 * first, 4 * (first + count), tail, 0, unroll=UNROLL)
 
     def back(u, s, first, count, begin=True):
         for n in range(first, first + count):
-            for c, group, size, place, tag in MESSAGES[s]:
+            for c in range(2):
                 dest = order[n] * 2 + c
-                src = y_out.at[n, pl.ds(group, size)]
-                dst = y_hbm.at[me, pl.ds(place, size)]
+                src = y_out.at[n, s + 3 * c]
+                dst = y_hbm.at[me, s]
 
                 @pl.when(dest != me)
                 def _():
-                    copy = remote(src, dst, ys_s.at[n, c, tag], ys_r.at[me, tag], row=dest)
+                    copy = remote(src, dst, ys_s.at[n, c, s], ys_r.at[me, s], row=dest)
                     copy.start() if begin else copy.wait_send()
 
                 @pl.when(dest == me)
                 def _():
-                    copy = pltpu.make_async_copy(src, dst, loc.at[6 + tag])
+                    copy = pltpu.make_async_copy(src, dst, loc.at[s, 3])
                     copy.start() if begin else copy.wait()
 
     units = [(0, 0, 0, col_count), (1, 1, 0, col_count), (2, 2, 0, col_count - 1), (3, 2, col_count - 1, 1)]
 
-    loads[0].wait()
+    def nothing():
+        pass
+
+    loaded(0)
     project(0, (0,), True)
     pl.semaphore_wait(barrier, row_count + 1)
     scatter_a(0)
     direct(0, 0, 1)
-    loads[1].wait()
-    project(1, (0,), True)
+    loaded(1)
+    project(1, (0,), True, (nothing, lambda: direct(0, 1, 2)))
     scatter_a(1)
-    direct(0, 1, 4)
-    project(0, (1,), False)
-    project(1, (1,), False)
-    direct(0, 4, 6)
-    loads[2].wait()
-    project(2, (0, 1), True)
+    project(0, (1,), False, (nothing, nothing, lambda: direct(0, 2, 4)))
+    project(1, (1,), False, (nothing, nothing, lambda: direct(0, 4, 6)))
+    loaded(2)
+    project(2, (0, 1), True, (nothing, nothing, lambda: direct(0, 6, row_count)))
     scatter_b()
     scatter_a(2)
     for copy in saves:
         copy.start()
-    direct(0, 6, row_count)
     forward(0, 0, row_count)
     direct(1, 0, row_count)
     forward(1, 0, row_count)
@@ -379,13 +403,10 @@
         copy.wait_send()
     for unit in units:
         back(*unit, begin=False)
-    for c in range(2):
-        @pl.when(core == c)
-        def _():
-            for q in range(1, row_count):
-                for tag, (place, size) in enumerate(ARRIVALS[c]):
-                    ref = y_hbm.at[peers[q], pl.ds(place, size)]
-                    remote(y_out.at[0, pl.ds(0, size)], ref, ys_s.at[0, 0, tag], ys_r.at[peers[q], tag], row=peers[q]).wait_recv()
+    for q in range(1, row_count):
+        for n in range(3):
+            ref = y_hbm.at[peers[q], n]
+            remote(y_out.at[0, 0], ref, ys_s.at[0, 0, n], ys_r.at[peers[q], n], row=peers[q]).wait_recv()
 
 
 def exchange(z, mask, g_in, w_a, w_ag, w_b, w_bg, g_out, row_count, col_count):
@@ -406,7 +427,7 @@
         out_specs=[hbm, hbm],
         out_shape=[
             jax.ShapeDtypeStruct((row_count, groups, 48, per, LANES), BF16),
-            jax.ShapeDtypeStruct((2, half, cols, chan), BF16),
+            jax.ShapeDtypeStruct((3, 2, half, HALF, chan), BF16),
         ],
         scratch_shapes=[
             pltpu.VMEM((3, 2, half, HALF, chan), BF16),
@@ -428,7 +449,7 @@
             dma((3, row_count)), dma((3, row_count)), dma((row_count,)), dma((row_count,)),
             dma((3, 2, row_count)), dma((3, 2, row_count)), dma((3, row_count)), dma((3, row_count)),
             dma((4, row_count)), dma((4, row_count)), dma((4, row_count)), dma((4, row_count)),
-            dma((col_count, 2, 2)), dma((row_count, 2)), dma((8,)),
+            dma((col_count, 2, 3)), dma((row_count, 3)), dma((3, 4)),
         ],
         compiler_params=pltpu.CompilerParams(collective_id=0, has_side_effects=True, vmem_limit_bytes=67000000),
         cost_estimate=pl.CostEstimate(flops=12 * per * depth * 2 * LANES * rows, bytes_accessed=z.size * 8, transcendentals=0),

time: 238 us -> 219 us (0.920)
  Pallas kernels: 238 us -> 217 us
    pallas_call x1, Pallas kernels: 220 us -> 207 us  [exchange(): pl.pallas_call(functools.partial(exchange_kernel, row_count, col_count),...]
    pallas_call x1, Pallas kernels: 18.4 us -> 9.75 us  [finish(): pl.pallas_call(finish_kernel, grid=(groups,), in_specs=[pl.BlockSpec((src...]
where the time goes in v5:
time: 219 us; the launch traced here: 217 us
  Pallas kernels  217 us (99%)
    pallas_call x1, Pallas kernels, exchange(): pl.pallas_call(functools.partial(exchange_kernel, row_count, col_count),...  207 us
    pallas_call x1, Pallas kernels, finish(): pl.pallas_call(finish_kernel, grid=(groups,), in_specs=[pl.BlockSpec((src...  9.75 us

profile of v5, /device:TPU:101, one launch (start us, length us, event | category | flops | bytes accessed | tf_op | source)
XLA Modules:
  0.0 216.8 jit_solution(13645088009361076748)
XLA Ops:
  0.0 207.0 %shard_map.100 = (bf16[8,3,48,16,128]{4,3,2,1,0:T(8,128)(2,1)}, bf16[3,2,48,64,128]{4,3,2,1,0:T(8,128)(2,1)}) custom-call(bf16[2,48,192,128]{3,2,1,0:T(8,128)(2,1)} %bitcast.4, s32[96,192]{1,0:T(8,128)} %m_ref.1, bf16[1,128]{1,0:T(2,128)(2,1)} %bitcast.6, bf16[128,128]{1,0:T(8,128)(2,1)} %wa_ref.1, bf16[128,128]{1,0:T(8,128)(2,1)} %wag_ref.1, ...), custom_call_target="tpu_custom_call" | custom-call | flops 4831838208 | bytes 18874368 | tf_op jit(solution)/shard_map/pallas_call | solution.py:424
  207.0 9.8 %shard_map.101 = bf16[96,192,128]{2,1,0:T(8,128)(2,1)} custom-call(bf16[8,3,48,16,128]{4,3,2,1,0:T(8,128)(2,1)} %get-tuple-element.7.y_ref, bf16[3,96,64,128]{3,2,1,0:T(8,128)(2,1)} %bitcast.5, bf16[96,192,128]{2,1,0:T(8,128)(2,1)} %z_ref.1, bf16[128,128]{1,0:T(8,128)(2,1)} %wg_ref.1, bf16[128,128]{1,0:T(8,128)(2,1)} %wo_ref.1), custom_call_target="tpu_custom_call" | custom-call | flops 1207959552 | bytes 18874368 | tf_op jit(solution)/shard_map/pallas_call | solution.py:71

commit v6 on v5

--- a/solution.py
+++ b/solution.py
@@ -93,8 +93,8 @@
 
 def exchange_kernel(
     row_count, col_count, z_hbm, m_ref, gi_ref, wa_ref, wag_ref, wb_ref, wbg_ref, go_ref, y_hbm, x_hbm,
-    zx, weights, keep, gains, turn, a_out, b_out, all_a, got_b, rhs, o_wide, o_tail, st_part, st_got, st_tot, y_out,
-    xa_s, xa_r, xb_s, xb_r, dir_s, dir_r, fwd_s, fwd_r, rs_s, rs_r, ag_s, ag_r, ys_s, ys_r, loc,
+    zx, weights, keep, gains, turn, a_out, b_out, all_a, got_b, rhs, o_wide, o_tail, st_part, st_pair, st_chip, st_got, st_far, st_tot, y_out,
+    xa_s, xa_r, xb_s, xb_r, dir_s, dir_r, fwd_s, fwd_r, pr_s, pr_r, rs_s, rs_r, ag_s, ag_r, sh_s, sh_r, ys_s, ys_r, loc,
 ):
     me, col = lax.axis_index('row'), lax.axis_index('col')
     per, _, half, _ = a_out.shape[1:]
@@ -109,6 +109,7 @@
     up, down = lax.rem(col + 1, col_count), lax.rem(col + col_count - 1, col_count)
     far = lax.rem(col + 2, col_count)
     order = (col, down, up, far)
+    alike = [q for q, (d, f) in enumerate(steps) if d and not f]
 
     loads = [
         [
@@ -167,7 +168,7 @@
                         flat_turn[pl.ds(side * heads * PITCH + t + r, heads, stride=PITCH), :] = act
                 return carry
 
-            lax.fori_loop(0, GROUP // PAIR, row, 0, unroll=2)
+            lax.fori_loop(0, GROUP // PAIR, row, 0, unroll=4)
 
             def pack(h, carry):
                 for side in sides:
@@ -185,10 +186,11 @@
         copy.start()
         sends.append(copy)
 
-    def scatter_a(s):
-        for q in range(1, row_count):
+    def scatter_a(s, first=1, last=row_count):
+        for q in range(first, last):
             send(a_out.at[peers[q], :, s], all_a.at[s, col, me], xa_s.at[s, q], xa_r.at[s, me], row=peers[q])
-        all_a[s, col, me] = a_out[me, :, s]
+        if first == 1:
+            all_a[s, col, me] = a_out[me, :, s]
 
     def scatter_b():
         for q in range(1, row_count):
@@ -267,42 +269,97 @@
             return carry
 
         lax.fori_loop(0, count * HALF // 8, tile, 0, unroll=UNROLL)
-        own = count * HALF // row_count
-        for q in range(1, row_count):
-            at = pl.ds(pl.multiple_of(first * HALF + own * peers[q], 8), own)
-            send(st_part.at[s, :, at], st_got.at[u, me, :, 0:own], rs_s.at[u, q], rs_r.at[u, me], row=peers[q])
+        if count == 1:
+            for q in range(1, row_count):
+                at = pl.ds(pl.multiple_of(first * HALF + 8 * peers[q], 8), 8)
+                send(st_part.at[s, :, at], st_far.at[me], rs_s.at[u, q], rs_r.at[u, me], row=peers[q])
+            return
+        size = count * HALF // 2
+        at = pl.ds(pl.multiple_of(first * HALF + size * (1 - core), 8), size)
+        send(st_part.at[s, :, at], st_pair.at[u, :, 0:size], pr_s.at[u], pr_r.at[u], row=peers[1])
+
+    def merge(u, s, first, count):
+        size = count * HALF // 2
+        own = size // chips
+        ref = st_pair.at[u, :, 0:size]
+        remote(ref, ref, pr_s.at[u], pr_r.at[u], row=peers[1]).wait_recv()
+
+        def tile(t, carry):
+            at = pl.ds(pl.multiple_of(8 * t, 8), 8)
+            mine = st_part[s, :, pl.ds(pl.multiple_of(first * HALF + size * core + 8 * t, 8), 8)]
+            other = st_pair[u, :, at]
+            total = mine + other
+            gap = (mine - other) ** 2 * (0.5 * per)
+            st_chip[u, 0, at] = 0.5 * total[0]
+            st_chip[u, 1, at] = total[1] + gap[0]
+            st_chip[u, 2, at] = jnp.where(lane < HALF, 0.5 * total[2], total[2] + swap(gap[2]))
+            return carry
+
+        lax.fori_loop(0, size // 8, tile, 0, unroll=UNROLL)
+        for q in alike:
+            at = pl.ds(pl.multiple_of(own * (peers[q] // 2), 8), own)
+            send(st_chip.at[u, :, at], st_got.at[u, chip, :, 0:own], rs_s.at[u, q], rs_r.at[u, chip], row=peers[q])
+
+    def settle(s, to, weight, means, squares, both):
+        parts = means.shape[0]
+        mean = jnp.sum(means, axis=0) * (1.0 / parts)
+        square = jnp.sum(squares, axis=0) + weight * jnp.sum((means - mean) ** 2, axis=0)
+        st_tot[s, 0, to] = mean
+        st_tot[s, 1, to] = lax.rsqrt(square * (1.0 / heads) + LN_EPS)
+        total = jnp.sum(both, axis=0)
+        mean = total * (1.0 / parts)
+        square = total + swap(weight * jnp.sum((both - mean) ** 2, axis=0))
+        st_tot[s, 2, to] = jnp.where(lane < HALF, mean, lax.rsqrt(square * (1.0 / heads) + LN_EPS))
 
     def combine(u, s, first, count):
-        own = count * HALF // row_count
-        base = pl.multiple_of(first * HALF + own * me, 8)
-        st_got[u, me, :, 0:own] = st_part[s, :, pl.ds(base, own)]
-        for q in range(1, row_count):
-            ref = st_got.at[u, peers[q], :, 0:own]
-            remote(ref, ref, rs_s.at[u, q], rs_r.at[u, peers[q]], row=peers[q]).wait_recv()
+        size = count * HALF // 2
+        own = size // chips
+        base = pl.multiple_of(first * HALF + size * core + own * chip, 8)
+        st_got[u, chip, :, 0:own] = st_chip[u, :, pl.ds(pl.multiple_of(own * chip, 8), own)]
+        for q in alike:
+            ref = st_got.at[u, peers[q] // 2, :, 0:own]
+            remote(ref, ref, rs_s.at[u, q], rs_r.at[u, peers[q] // 2], row=peers[q]).wait_recv()
         for t in range(own // 8):
             at = slice(8 * t, 8 * t + 8)
-            to = pl.ds(pl.multiple_of(base + 8 * t, 8), 8)
-            means, squares, both = st_got[u, :, 0, at], st_got[u, :, 1, at], st_got[u, :, 2, at]
-            mean = jnp.sum(means, axis=0) * (1.0 / row_count)
-            square = jnp.sum(squares, axis=0) + per * jnp.sum((means - mean) ** 2, axis=0)
-            st_tot[s, 0, to] = mean
-            st_tot[s, 1, to] = lax.rsqrt(square * (1.0 / heads) + LN_EPS)
-            total = jnp.sum(both, axis=0)
-            mean = total * (1.0 / row_count)
-            square = total + swap(per * jnp.sum((both - mean) ** 2, axis=0))
-            st_tot[s, 2, to] = jnp.where(lane < HALF, mean, lax.rsqrt(square * (1.0 / heads) + LN_EPS))
+            settle(s, pl.ds(pl.multiple_of(base + 8 * t, 8), 8), 2 * per, *(st_got[u, :, n, at] for n in range(3)))
+        for q in alike:
+            ref = st_tot.at[s, :, pl.ds(base, own)]
+            send(ref, ref, ag_s.at[u, q], ag_r.at[u, chip], row=peers[q])
+
+    def combine_far(u, s, first, count):
+        base = pl.multiple_of(first * HALF + 8 * me, 8)
+        at = pl.ds(base, 8)
+        st_far[me] = st_part[s, :, at]
         for q in range(1, row_count):
-            ref = st_tot.at[s, :, pl.ds(base, own)]
+            ref = st_far.at[peers[q]]
+            remote(ref, ref, rs_s.at[u, q], rs_r.at[u, peers[q]], row=peers[q]).wait_recv()
+        settle(s, at, per, *(st_far[:, n] for n in range(3)))
+        for q in range(1, row_count):
+            ref = st_tot.at[s, :, at]
             send(ref, ref, ag_s.at[u, q], ag_r.at[u, me], row=peers[q])
+
+    def share(u, s, first, count):
+        size = count * HALF // 2
+        own = size // chips
+        base = first * HALF + size * core
+        for q in alike:
+            ref = st_tot.at[s, :, pl.ds(pl.multiple_of(base + own * (peers[q] // 2), 8), own)]
+            remote(ref, ref, ag_s.at[u, q], ag_r.at[u, peers[q] // 2], row=peers[q]).wait_recv()
+        ref = st_tot.at[s, :, pl.ds(pl.multiple_of(base, 8), size)]
+        send(ref, ref, sh_s.at[u], sh_r.at[u], row=peers[1])
 
     gain_out = gains[pl.ds(pl.multiple_of(me * per, 8), per), :]
     low = lax.broadcasted_iota(jnp.int32, (per, LANES), 1) < HALF
 
     def normalize(u, s, first, count):
-        own = count * HALF // row_count
-        for q in range(1, row_count):
-            ref = st_tot.at[s, :, pl.ds(pl.multiple_of(first * HALF + own * peers[q], 8), own)]
-            remote(ref, ref, ag_s.at[u, q], ag_r.at[u, peers[q]], row=peers[q]).wait_recv()
+        if count == 1:
+            for q in range(1, row_count):
+                ref = st_tot.at[s, :, pl.ds(pl.multiple_of(first * HALF + 8 * peers[q], 8), 8)]
+                remote(ref, ref, ag_s.at[u, q], ag_r.at[u, peers[q]], row=peers[q]).wait_recv()
+        else:
+            size = count * HALF // 2
+            ref = st_tot.at[s, :, pl.ds(pl.multiple_of(first * HALF + size * (1 - core), 8), size)]
+            remote(ref, ref, sh_s.at[u], sh_r.at[u], row=peers[1]).wait_recv()
         base = (s % 2) * (per * pitch)
 
         def wide(t, carry):
@@ -328,9 +385,9 @@
         lax.fori_loop(8 * first, 8 * (first + count), wide, 0, unroll=UNROLL)
         lax.fori_loop(4 * first, 4 * (first + count), tail, 0, unroll=UNROLL)
 
-    def back(u, s, first, count, begin=True):
-        for n in range(first, first + count):
-            for c in range(2):
+    def back(u, s, first, count, begin=True, cores=(0, 1)):
+        for c in cores:
+            for n in range(first, first + count):
                 dest = order[n] * 2 + c
                 src = y_out.at[n, s + 3 * c]
                 dst = y_hbm.at[me, s]
@@ -363,7 +420,7 @@
     loaded(2)
     project(2, (0, 1), True, (nothing, nothing, lambda: direct(0, 6, row_count)))
     scatter_b()
-    scatter_a(2)
+    scatter_a(2, 1, row_count)
     for copy in saves:
         copy.start()
     forward(0, 0, row_count)
@@ -373,26 +430,34 @@
     arrived(0)
     product(*units[0])
     partial(*units[0])
+    merge(*units[0])
     direct(2, 0, row_count)
     combine(*units[0])
     arrived(1)
     product(*units[1])
     partial(*units[1])
+    share(*units[0])
+    merge(*units[1])
     normalize(*units[0])
+    back(*units[0], cores=(0,))
     combine(*units[1])
-    back(*units[0])
-    forward(2, 0, row_count // 2)
+    back(*units[0], cores=(1,))
+    share(*units[1])
+    forward(2, 0, 4)
     normalize(*units[1])
-    back(*units[1])
-    forward(2, row_count // 2, row_count)
+    back(*units[1], cores=(0,))
+    forward(2, 4, 8)
     product(*units[2])
     partial(*units[2])
+    merge(*units[2])
     combine(*units[2])
+    back(*units[1], cores=(1,))
+    share(*units[2])
     arrived(2)
     product(*units[3])
     partial(*units[3])
     normalize(*units[2])
-    combine(*units[3])
+    combine_far(*units[3])
     back(*units[2])
     normalize(*units[3])
     back(*units[3])
@@ -443,12 +508,15 @@
             pltpu.VMEM((2, per, rows + 8, LANES), F32),
             pltpu.VMEM((2, per, rows + 8, LANES), F32),
             pltpu.VMEM((3, 3, rows, LANES), F32),
-            pltpu.VMEM((4, row_count, 3, rows // row_count, LANES), F32),
+            pltpu.VMEM((3, 3, rows // 2, LANES), F32),
+            pltpu.VMEM((3, 3, rows // 2, LANES), F32),
+            pltpu.VMEM((3, row_count // 2, 3, rows // row_count, LANES), F32),
+            pltpu.VMEM((row_count, 3, 8, LANES), F32),
             pltpu.VMEM((3, 3, rows, LANES), F32),
             pltpu.VMEM((col_count, 2 * groups, 48, per, LANES), BF16),
             dma((3, row_count)), dma((3, row_count)), dma((row_count,)), dma((row_count,)),
             dma((3, 2, row_count)), dma((3, 2, row_count)), dma((3, row_count)), dma((3, row_count)),
-            dma((4, row_count)), dma((4, row_count)), dma((4, row_count)), dma((4, row_count)),
+            dma((4,)), dma((4,)), dma((4, row_count)), dma((4, row_count)), dma((4, row_count)), dma((4, row_count)), dma((4,)), dma((4,)),
             dma((col_count, 2, 3)), dma((row_count, 3)), dma((3, 4)),
         ],
         compiler_params=pltpu.CompilerParams(collective_id=0, has_side_effects=True, vmem_limit_bytes=67000000),

time: 219 us -> 208 us (0.950); the launches traced: 217 us -> 208 us
  Pallas kernels: 217 us -> 208 us
    pallas_call x1, Pallas kernels: 207 us -> 199 us  [exchange(): pl.pallas_call(functools.partial(exchange_kernel, row_count, col_count),...]
where the time goes in v6:
time: 208 us
  Pallas kernels  208 us (100%)
    pallas_call x1, Pallas kernels, exchange(): pl.pallas_call(functools.partial(exchange_kernel, row_count, col_count),...  199 us
    pallas_call x1, Pallas kernels, finish(): pl.pallas_call(finish_kernel, grid=(groups,), in_specs=[pl.BlockSpec((src...  9.75 us

profile of v6, /device:TPU:101, one launch (start us, length us, event | category | flops | bytes accessed | tf_op | source)
XLA Modules:
  0.0 208.3 jit_solution(14900941446272045684)
XLA Ops:
  0.0 198.6 %shard_map.100 = (bf16[8,3,48,16,128]{4,3,2,1,0:T(8,128)(2,1)}, bf16[3,2,48,64,128]{4,3,2,1,0:T(8,128)(2,1)}) custom-call(bf16[2,48,192,128]{3,2,1,0:T(8,128)(2,1)} %bitcast.4, s32[96,192]{1,0:T(8,128)} %m_ref.1, bf16[1,128]{1,0:T(2,128)(2,1)} %bitcast.6, bf16[128,128]{1,0:T(8,128)(2,1)} %wa_ref.1, bf16[128,128]{1,0:T(8,128)(2,1)} %wag_ref.1, ...), custom_call_target="tpu_custom_call" | custom-call | flops 4831838208 | bytes 18874368 | tf_op jit(solution)/shard_map/pallas_call | solution.py:489
  198.6 9.7 %shard_map.101 = bf16[96,192,128]{2,1,0:T(8,128)(2,1)} custom-call(bf16[8,3,48,16,128]{4,3,2,1,0:T(8,128)(2,1)} %get-tuple-element.7.y_ref, bf16[3,96,64,128]{3,2,1,0:T(8,128)(2,1)} %bitcast.5, bf16[96,192,128]{2,1,0:T(8,128)(2,1)} %z_ref.1, bf16[128,128]{1,0:T(8,128)(2,1)} %wg_ref.1, bf16[128,128]{1,0:T(8,128)(2,1)} %wo_ref.1), custom_call_target="tpu_custom_call" | custom-call | flops 1207959552 | bytes 18874368 | tf_op jit(solution)/shard_map/pallas_call | solution.py:71

commit v7 on v6

--- a/solution.py
+++ b/solution.py
@@ -12,7 +12,7 @@
 HALF = 64
 GROUP = 16
 PITCH = 24
-BATCH = 16
+BATCH = 32
 QUART = 32
 PAIR = 2
 UNROLL = 4
@@ -148,12 +148,12 @@
     def project(s, sides, fresh, between=()):
         if fresh:
             def norm(i, carry):
-                at = pl.ds(4 * i, 4)
-                v = zx[s, :, at].astype(F32).reshape(4 * LANES, heads)
-                zx[s, :, at] = layer_norm(v, gain_in).astype(BF16).reshape(2, 4, HALF, heads)
+                at = pl.ds(8 * i, 8)
+                v = zx[s, :, at].astype(F32).reshape(8 * LANES, heads)
+                zx[s, :, at] = layer_norm(v, gain_in).astype(BF16).reshape(2, 8, HALF, heads)
                 return carry
 
-            lax.fori_loop(0, half // 4, norm, 0)
+            lax.fori_loop(0, half // 8, norm, 0)
 
         for g in range(half // GROUP):
             def row(i, carry):
@@ -168,14 +168,14 @@
                         flat_turn[pl.ds(side * heads * PITCH + t + r, heads, stride=PITCH), :] = act
                 return carry
 
-            lax.fori_loop(0, GROUP // PAIR, row, 0, unroll=4)
+            lax.fori_loop(0, GROUP // PAIR, row, 0, unroll=8)
 
             def pack(h, carry):
                 for side in sides:
                     flat_out[side][h, s, g * GROUP:(g + 1) * GROUP] = turn[side * heads + h, 0:GROUP].astype(BF16)
                 return carry
 
-            lax.fori_loop(0, heads, pack, 0, unroll=8)
+            lax.fori_loop(0, heads, pack, 0, unroll=32)
             if g < len(between):
                 between[g]()
 

time: 208 us -> 206 us (level)
  no operation moved by 1% of the time
where the time goes in v7:
time: 206 us
  Pallas kernels  206 us (100%)
    pallas_call x1, Pallas kernels, exchange(): pl.pallas_call(functools.partial(exchange_kernel, row_count, col_count),...  197 us
    pallas_call x1, Pallas kernels, finish(): pl.pallas_call(finish_kernel, grid=(groups,), in_specs=[pl.BlockSpec((src...  9.14 us

profile of v7, /device:TPU:101, one launch (start us, length us, event | category | flops | bytes accessed | tf_op | source)
XLA Modules:
  0.0 206.3 jit_solution(13493989816588501323)
XLA Ops:
  0.0 197.2 %shard_map.100 = (bf16[8,3,48,16,128]{4,3,2,1,0:T(8,128)(2,1)}, bf16[3,2,48,64,128]{4,3,2,1,0:T(8,128)(2,1)}) custom-call(bf16[2,48,192,128]{3,2,1,0:T(8,128)(2,1)} %bitcast.4, s32[96,192]{1,0:T(8,128)} %m_ref.1, bf16[1,128]{1,0:T(2,128)(2,1)} %bitcast.6, bf16[128,128]{1,0:T(8,128)(2,1)} %wa_ref.1, bf16[128,128]{1,0:T(8,128)(2,1)} %wag_ref.1, ...), custom_call_target="tpu_custom_call" | custom-call | flops 4831838208 | bytes 18874368 | tf_op jit(solution)/shard_map/pallas_call | solution.py:489
  197.2 9.1 %shard_map.101 = bf16[96,192,128]{2,1,0:T(8,128)(2,1)} custom-call(bf16[8,3,48,16,128]{4,3,2,1,0:T(8,128)(2,1)} %get-tuple-element.7.y_ref, bf16[3,96,64,128]{3,2,1,0:T(8,128)(2,1)} %bitcast.5, bf16[96,192,128]{2,1,0:T(8,128)(2,1)} %z_ref.1, bf16[128,128]{1,0:T(8,128)(2,1)} %wg_ref.1, bf16[128,128]{1,0:T(8,128)(2,1)} %wo_ref.1), custom_call_target="tpu_custom_call" | custom-call | flops 1207959552 | bytes 18874368 | tf_op jit(solution)/shard_map/pallas_call | solution.py:71

commit v8 on v7

--- a/solution.py
+++ b/solution.py
@@ -22,6 +22,10 @@
 
 def dot(lhs, rhs, dims):
     return lax.dot_general(lhs, rhs, (dims, ((), ())), preferred_element_type=F32)
+
+
+def loop(count, body, **options):
+    lax.fori_loop(0, count, body, 0, **options)
 
 
 def layer_norm(values, gain):
@@ -52,7 +56,7 @@
             out_ref[at, part] = res[:, QUART * e:QUART * (e + 1)]
         return carry
 
-    lax.fori_loop(0, 32 // BATCH, wide, 0)
+    loop(32 // BATCH, wide)
     turned = jnp.concatenate([y_ref[:, 0, 32 + r].reshape(heads, LANES) for r in range(16)], axis=1)
     upd = dot(turned, wo_ref[...], ((0,), (0,)))
     rows = [r + 16 * h for r in range(16) for h in range(2)]
@@ -153,7 +157,7 @@
                 zx[s, :, at] = layer_norm(v, gain_in).astype(BF16).reshape(2, 8, HALF, heads)
                 return carry
 
-            lax.fori_loop(0, half // 8, norm, 0)
+            loop(half // 8, norm)
 
         for g in range(half // GROUP):
             def row(i, carry):
@@ -168,14 +172,14 @@
                         flat_turn[pl.ds(side * heads * PITCH + t + r, heads, stride=PITCH), :] = act
                 return carry
 
-            lax.fori_loop(0, GROUP // PAIR, row, 0, unroll=8)
+            loop(GROUP // PAIR, row, unroll=8)
 
             def pack(h, carry):
                 for side in sides:
                     flat_out[side][h, s, g * GROUP:(g + 1) * GROUP] = turn[side * heads + h, 0:GROUP].astype(BF16)
                 return carry
 
-            lax.fori_loop(0, heads, pack, 0, unroll=32)
+            loop(heads, pack, unroll=32)
             if g < len(between):
                 between[g]()
 
@@ -240,7 +244,7 @@
             rhs[h, 1, :, LANES:] = jnp.concatenate([w[2][:, HALF:], w[2][:, :HALF]], axis=1)
             return carry
 
-        lax.fori_loop(0, per, channel, 0, unroll=UNROLL)
+        loop(per, channel, unroll=UNROLL)
 
     def product(u, s, first, count):
         at = slice(first * HALF, (first + count) * HALF)
@@ -253,7 +257,7 @@
             o_tail[s % 2, h, at] = res[:, LANES:]
             return carry
 
-        lax.fori_loop(0, per, channel, 0, unroll=UNROLL)
+        loop(per, channel, unroll=UNROLL)
 
     def partial(u, s, first, count):
         def tile(t, carry):
@@ -268,7 +272,7 @@
             st_part[s, 2, at] = jnp.where(lane < HALF, out[2], swap(out[3]))
             return carry
 
-        lax.fori_loop(0, count * HALF // 8, tile, 0, unroll=UNROLL)
+        loop(count * HALF // 8, tile, unroll=UNROLL)
         if count == 1:
             for q in range(1, row_count):
                 at = pl.ds(pl.multiple_of(first * HALF + 8 * peers[q], 8), 8)
@@ -295,7 +299,7 @@
             st_chip[u, 2, at] = jnp.where(lane < HALF, 0.5 * total[2], total[2] + swap(gap[2]))
             return carry
 
-        lax.fori_loop(0, size // 8, tile, 0, unroll=UNROLL)
+        loop(size // 8, tile, unroll=UNROLL)
         for q in alike:
             at = pl.ds(pl.multiple_of(own * (peers[q] // 2), 8), own)
             send(st_chip.at[u, :, at], st_got.at[u, chip, :, 0:own], rs_s.at[u, q], rs_r.at[u, chip], row=peers[q])
@@ -484,6 +488,9 @@
     groups = tile_rows // 32
     wire = (row_count, per, 3, half, LANES)
     dma = pltpu.SemaphoreType.DMA
+    chunk_sem, ways_sem, unit_sem, peer_sem = dma((3, row_count)), dma((3, 2, row_count)), dma((4,)), dma((4, row_count))
+    o_buffer = pltpu.VMEM((2, per, rows + 8, LANES), F32)
+    st_buffer, st_halves = pltpu.VMEM((3, 3, rows, LANES), F32), pltpu.VMEM((3, 3, rows // 2, LANES), F32)
     hbm = pl.BlockSpec(memory_space=pl.ANY)
     vmem = pl.BlockSpec(memory_space=pltpu.VMEM)
     return pl.pallas_call(
@@ -505,18 +512,18 @@
             pltpu.VMEM((3, col_count, row_count, per, half, LANES), BF16),
             pltpu.VMEM(wire, BF16),
             pltpu.VMEM((per, 2, depth, 2 * LANES), BF16),
-            pltpu.VMEM((2, per, rows + 8, LANES), F32),
-            pltpu.VMEM((2, per, rows + 8, LANES), F32),
-            pltpu.VMEM((3, 3, rows, LANES), F32),
-            pltpu.VMEM((3, 3, rows // 2, LANES), F32),
-            pltpu.VMEM((3, 3, rows // 2, LANES), F32),
+            o_buffer,
+            o_buffer,
+            st_buffer,
+            st_halves,
+            st_halves,
             pltpu.VMEM((3, row_count // 2, 3, rows // row_count, LANES), F32),
             pltpu.VMEM((row_count, 3, 8, LANES), F32),
-            pltpu.VMEM((3, 3, rows, LANES), F32),
+            st_buffer,
             pltpu.VMEM((col_count, 2 * groups, 48, per, LANES), BF16),
-            dma((3, row_count)), dma((3, row_count)), dma((row_count,)), dma((row_count,)),
-            dma((3, 2, row_count)), dma((3, 2, row_count)), dma((3, row_count)), dma((3, row_count)),
-            dma((4,)), dma((4,)), dma((4, row_count)), dma((4, row_count)), dma((4, row_count)), dma((4, row_count)), dma((4,)), dma((4,)),
+            chunk_sem, chunk_sem, dma((row_count,)), dma((row_count,)),
+            ways_sem, ways_sem, chunk_sem, chunk_sem,
+            unit_sem, unit_sem, peer_sem, peer_sem, peer_sem, peer_sem, unit_sem, unit_sem,
             dma((col_count, 2, 3)), dma((row_count, 3)), dma((3, 4)),
         ],
         compiler_params=pltpu.CompilerParams(collective_id=0, has_side_effects=True, vmem_limit_bytes=67000000),

time: 206 us -> 206 us (level)
  no operation moved by 1% of the time
where the time goes in v8:
time: 206 us
  Pallas kernels  206 us (100%)
    pallas_call x1, Pallas kernels, exchange(): pl.pallas_call(functools.partial(exchange_kernel, row_count, col_count),...  197 us
    pallas_call x1, Pallas kernels, finish(): pl.pallas_call(finish_kernel, grid=(groups,), in_specs=[pl.BlockSpec((src...  9.14 us

profile of v8, /device:TPU:101, one launch (start us, length us, event | category | flops | bytes accessed | tf_op | source)
XLA Modules:
  0.0 206.3 jit_solution(13493989816588501323)
XLA Ops:
  0.0 197.2 %shard_map.100 = (bf16[8,3,48,16,128]{4,3,2,1,0:T(8,128)(2,1)}, bf16[3,2,48,64,128]{4,3,2,1,0:T(8,128)(2,1)}) custom-call(bf16[2,48,192,128]{3,2,1,0:T(8,128)(2,1)} %bitcast.4, s32[96,192]{1,0:T(8,128)} %m_ref.1, bf16[1,128]{1,0:T(2,128)(2,1)} %bitcast.6, bf16[128,128]{1,0:T(8,128)(2,1)} %wa_ref.1, bf16[128,128]{1,0:T(8,128)(2,1)} %wag_ref.1, ...), custom_call_target="tpu_custom_call" | custom-call | flops 4831838208 | bytes 18874368 | tf_op jit(solution)/shard_map/pallas_call | solution.py:496
  197.2 9.1 %shard_map.101 = bf16[96,192,128]{2,1,0:T(8,128)(2,1)} custom-call(bf16[8,3,48,16,128]{4,3,2,1,0:T(8,128)(2,1)} %get-tuple-element.7.y_ref, bf16[3,96,64,128]{3,2,1,0:T(8,128)(2,1)} %bitcast.5, bf16[96,192,128]{2,1,0:T(8,128)(2,1)} %z_ref.1, bf16[128,128]{1,0:T(8,128)(2,1)} %wg_ref.1, bf16[128,128]{1,0:T(8,128)(2,1)} %wo_ref.1), custom_call_target="tpu_custom_call" | custom-call | flops 1207959552 | bytes 18874368 | tf_op jit(solution)/shard_map/pallas_call | solution.py:75

commit v9 on v8

--- a/solution.py
+++ b/solution.py
@@ -112,8 +112,8 @@
     peers = [lax.rem(chip + d + chips, chips) * 2 + lax.rem(core + f, 2) for d, f in steps]
     up, down = lax.rem(col + 1, col_count), lax.rem(col + col_count - 1, col_count)
     far = lax.rem(col + 2, col_count)
-    order = (col, down, up, far)
-    alike = [q for q, (d, f) in enumerate(steps) if d and not f]
+    order = (col, up, down, far)
+    alike = [q for q, (d, f) in enumerate(steps) if d and not f][::-1]
 
     loads = [
         [
@@ -274,7 +274,7 @@
 
         loop(count * HALF // 8, tile, unroll=UNROLL)
         if count == 1:
-            for q in range(1, row_count):
+            for q in reversed(range(1, row_count)):
                 at = pl.ds(pl.multiple_of(first * HALF + 8 * peers[q], 8), 8)
                 send(st_part.at[s, :, at], st_far.at[me], rs_s.at[u, q], rs_r.at[u, me], row=peers[q])
             return
@@ -338,7 +338,7 @@
             ref = st_far.at[peers[q]]
             remote(ref, ref, rs_s.at[u, q], rs_r.at[u, peers[q]], row=peers[q]).wait_recv()
         settle(s, at, per, *(st_far[:, n] for n in range(3)))
-        for q in range(1, row_count):
+        for q in reversed(range(1, row_count)):
             ref = st_tot.at[s, :, at]
             send(ref, ref, ag_s.at[u, q], ag_r.at[u, me], row=peers[q])
 
@@ -390,9 +390,14 @@
         lax.fori_loop(4 * first, 4 * (first + count), tail, 0, unroll=UNROLL)
 
     def back(u, s, first, count, begin=True, cores=(0, 1)):
+        if count == col_count:
+            gaps = [lax.rem(chip + d + col_count - col, col_count) for d in (1, 3, 2, 0)]
+            places = [(d + d // 2 - 2 * (d // 3), lax.rem(col + d, col_count)) for d in gaps]
+        else:
+            places = [(n, order[n]) for n in range(first, first + count)]
         for c in cores:
-            for n in range(first, first + count):
-                dest = order[n] * 2 + c
+            for n, block in places:
+                dest = block * 2 + c
                 src = y_out.at[n, s + 3 * c]
                 dst = y_hbm.at[me, s]
 

time: 206 us -> 207 us (level)
  no operation moved by 1% of the time
where the time goes in v9:
time: 207 us
  Pallas kernels  207 us (100%)
    pallas_call x1, Pallas kernels, exchange(): pl.pallas_call(functools.partial(exchange_kernel, row_count, col_count),...  198 us
    pallas_call x1, Pallas kernels, finish(): pl.pallas_call(finish_kernel, grid=(groups,), in_specs=[pl.BlockSpec((src...  9.13 us

profile of v9, /device:TPU:101, one launch (start us, length us, event | category | flops | bytes accessed | tf_op | source)
XLA Modules:
  0.0 207.0 jit_solution(10857684677219937517)
XLA Ops:
  0.0 197.8 %shard_map.100 = (bf16[8,3,48,16,128]{4,3,2,1,0:T(8,128)(2,1)}, bf16[3,2,48,64,128]{4,3,2,1,0:T(8,128)(2,1)}) custom-call(bf16[2,48,192,128]{3,2,1,0:T(8,128)(2,1)} %bitcast.4, s32[96,192]{1,0:T(8,128)} %m_ref.1, bf16[1,128]{1,0:T(2,128)(2,1)} %bitcast.6, bf16[128,128]{1,0:T(8,128)(2,1)} %wa_ref.1, bf16[128,128]{1,0:T(8,128)(2,1)} %wag_ref.1, ...), custom_call_target="tpu_custom_call" | custom-call | flops 4831838208 | bytes 18874368 | tf_op jit(solution)/shard_map/pallas_call | solution.py:501
  197.9 9.1 %shard_map.101 = bf16[96,192,128]{2,1,0:T(8,128)(2,1)} custom-call(bf16[8,3,48,16,128]{4,3,2,1,0:T(8,128)(2,1)} %get-tuple-element.7.y_ref, bf16[3,96,64,128]{3,2,1,0:T(8,128)(2,1)} %bitcast.5, bf16[96,192,128]{2,1,0:T(8,128)(2,1)} %z_ref.1, bf16[128,128]{1,0:T(8,128)(2,1)} %wg_ref.1, bf16[128,128]{1,0:T(8,128)(2,1)} %wo_ref.1), custom_call_target="tpu_custom_call" | custom-call | flops 1207959552 | bytes 18874368 | tf_op jit(solution)/shard_map/pallas_call | solution.py:75
